TPU v7x, 32 devices: a whole 2x2x4 slice. The times are simulated.
32 devices in a mesh: dp: 8 (over y, x, core), tensor: 4 (over z).
Axes of the slice: x: 2, y: 2, z: 4, core: 2. Of those that a mesh axis runs over, the one named last changes fastest.
Arguments:
- tokens: bfloat16 [8192, 1024], P(('dp', 'tensor')), may hold values from -6 to 6
- segment_ids: int32 [8, 1024], P('dp'), may hold values from 0 to 7, never falling along the last dimension, each value on 1 to 512 neighbouring positions
- out_grad: bfloat16 [8192, 1024], P(('dp', 'tensor')), may hold values from -6 to 6
- w_qkv: bfloat16 [1024, 3, 1024], P('dp', None, 'tensor'), may hold values from -0.1875 to 0.1875
- b_qv: bfloat16 [2, 1024], P(None, 'tensor'), may hold values from -3 to 3
- w_out: bfloat16 [1024, 1024], P('tensor', 'dp'), may hold values from -1.5 to 1.5
- b_out: bfloat16 [1024], replicated, may hold values from -3 to 3
- norm1_gain: bfloat16 [1024], replicated, may hold values from 0.099609375 to 1.8984375
- norm1_bias: bfloat16 [1024], replicated, may hold values from -3 to 3
- w_up: bfloat16 [1024, 4096], P('dp', 'tensor'), may hold values from -0.1875 to 0.1875
- b_up: bfloat16 [4096], P('tensor'), may hold values from -3 to 3
- w_down: bfloat16 [4096, 1024], P('tensor', 'dp'), may hold values from -0.09375 to 0.09375
- b_down: bfloat16 [1024], replicated, may hold values from -3 to 3
- norm2_gain: bfloat16 [1024], replicated, may hold values from 0.099609375 to 1.8984375
- norm2_bias: bfloat16 [1024], replicated, may hold values from -3 to 3
Outputs:
- output: bfloat16 [8192, 1024], P(('dp', 'tensor'))
- grad_tokens: bfloat16 [8192, 1024], P(('dp', 'tensor'))
- grad_w_qkv: float32 [1024, 3, 1024], P('dp', None, 'tensor')
- grad_b_qv: float32 [2, 1024], P(None, 'tensor')
- grad_w_out: float32 [1024, 1024], P('tensor', 'dp')
- grad_b_out: float32 [1024], replicated
- grad_norm1_gain: float32 [1024], replicated
- grad_norm1_bias: float32 [1024], replicated
- grad_w_up: float32 [1024, 4096], P('dp', 'tensor')
- grad_b_up: float32 [4096], P('tensor')
- grad_w_down: float32 [4096, 1024], P('tensor', 'dp')
- grad_b_down: float32 [1024], replicated
- grad_norm2_gain: float32 [1024], replicated
- grad_norm2_bias: float32 [1024], replicated
Inputs may be any that keep to these rules, and one draw needn't show every extreme that they name: `segment_ids`: along each packed row the ids never fall; each id covers one run of 1 to 512 positions, and some run in each row has exactly 512.
All inputs are finite; a program needn't handle non-finite values.
Results may differ from a plain program's by a relative error of at most 0.02.
Values may be sent and summed in bfloat16 or wider, within the bound.
A program may use at most 128 MiB of HBM per device.

v0:
```python
import math

import jax
import jax.numpy as jnp
from jax import lax
from jax.sharding import PartitionSpec as P

HD = 64


def rows_product(left_side, right_side):
    return lax.dot_general(
        left_side, right_side, (((0,), (0,)), ((), ())), preferred_element_type=jnp.float32
    )


def transposed(left_side, right_side):
    return lax.dot_general(
        left_side, right_side, (((1,), (1,)), ((), ())), preferred_element_type=jnp.float32
    )


def norm_forward(summed, norm_gain, norm_bias):
    row_mean = jnp.mean(summed, axis=-1, keepdims=True)
    centred = summed - row_mean
    inverse = lax.rsqrt(jnp.mean(centred * centred, axis=-1, keepdims=True) + 1e-05)
    normed = centred * inverse
    return (normed * norm_gain + norm_bias, normed, inverse)


def norm_backward(upstream, norm_gain, normed, inverse):
    scaled = upstream * norm_gain
    return inverse * (
        scaled
        - jnp.mean(scaled, axis=-1, keepdims=True)
        - normed * jnp.mean(scaled * normed, axis=-1, keepdims=True)
    )


def gelu_slope(values):
    return 0.5 * (1.0 + lax.erf(values * 2.0 ** (-0.5))) + values * jnp.exp(
        -0.5 * values * values
    ) * (2.0 * math.pi) ** (-0.5)


def block_scores(query_block, key_window, seg_query, seg_window):
    scores = jnp.einsum(
        "qhd,khd->hqk", query_block, key_window, preferred_element_type=jnp.float32
    ) * HD ** (-0.5)
    same_doc = seg_query[:, None] == seg_window[None, :]
    return jnp.where(same_doc[None], scores, -1e30)


def padded_inputs(key_heads, value_heads, segments, block_size):
    padding = ((block_size, block_size), (0, 0), (0, 0))
    seg_padded = jnp.pad(segments, (block_size, block_size), constant_values=-1)
    return (jnp.pad(key_heads, padding), jnp.pad(value_heads, padding), seg_padded)


def attention_forward(query_heads, key_heads, value_heads, segments):
    row_count = query_heads.shape[0]
    block_size = min(512, row_count)
    key_padded, value_padded, seg_padded = padded_inputs(
        key_heads, value_heads, segments, block_size
    )

    def one_block(block_index):
        offset = block_index * block_size
        query_block = lax.dynamic_slice_in_dim(query_heads, offset, block_size, 0)
        key_window = lax.dynamic_slice_in_dim(key_padded, offset, 3 * block_size, 0)
        value_window = lax.dynamic_slice_in_dim(value_padded, offset, 3 * block_size, 0)
        seg_query = lax.dynamic_slice_in_dim(segments, offset, block_size, 0)
        seg_window = lax.dynamic_slice_in_dim(seg_padded, offset, 3 * block_size, 0)
        scores = block_scores(query_block, key_window, seg_query, seg_window)
        row_max = jnp.max(scores, axis=-1, keepdims=True)
        expd = jnp.exp(scores - row_max)
        totals = jnp.sum(expd, axis=-1, keepdims=True)
        attn_probs = (expd / totals).astype(jnp.bfloat16)
        context = jnp.einsum(
            "hqk,khd->qhd", attn_probs, value_window, preferred_element_type=jnp.float32
        )
        return (context.astype(jnp.bfloat16), (row_max + jnp.log(totals))[..., 0])

    context, log_totals = lax.map(one_block, jnp.arange(row_count // block_size))
    return (context.reshape(query_heads.shape), log_totals)


def attention_backward(query_heads, key_heads, value_heads, segments, log_totals, grad_context):
    row_count = query_heads.shape[0]
    block_size = min(512, row_count)
    key_padded, value_padded, seg_padded = padded_inputs(
        key_heads, value_heads, segments, block_size
    )
    scale = HD ** (-0.5)
    acc_shape = key_padded.shape

    def one_block(block_index, loop_state):
        key_acc, value_acc, query_acc = loop_state
        offset = block_index * block_size
        query_block = lax.dynamic_slice_in_dim(query_heads, offset, block_size, 0)
        grad_block = lax.dynamic_slice_in_dim(grad_context, offset, block_size, 0)
        key_window = lax.dynamic_slice_in_dim(key_padded, offset, 3 * block_size, 0)
        value_window = lax.dynamic_slice_in_dim(value_padded, offset, 3 * block_size, 0)
        seg_query = lax.dynamic_slice_in_dim(segments, offset, block_size, 0)
        seg_window = lax.dynamic_slice_in_dim(seg_padded, offset, 3 * block_size, 0)
        scores = block_scores(query_block, key_window, seg_query, seg_window)
        attn_probs = jnp.exp(scores - log_totals[block_index][..., None])
        grad_probs = jnp.einsum(
            "qhd,khd->hqk", grad_block, value_window, preferred_element_type=jnp.float32
        )
        row_delta = jnp.sum(attn_probs * grad_probs, axis=-1, keepdims=True)
        grad_scores = (attn_probs * (grad_probs - row_delta)).astype(jnp.bfloat16)
        grad_query = (
            jnp.einsum("hqk,khd->qhd", grad_scores, key_window, preferred_element_type=jnp.float32)
            * scale
        )
        grad_keys = (
            jnp.einsum("hqk,qhd->khd", grad_scores, query_block, preferred_element_type=jnp.float32)
            * scale
        )
        grad_values = jnp.einsum(
            "hqk,qhd->khd",
            attn_probs.astype(jnp.bfloat16),
            grad_block,
            preferred_element_type=jnp.float32,
        )
        key_acc = lax.dynamic_update_slice_in_dim(
            key_acc,
            lax.dynamic_slice_in_dim(key_acc, offset, 3 * block_size, 0) + grad_keys,
            offset,
            0,
        )
        value_acc = lax.dynamic_update_slice_in_dim(
            value_acc,
            lax.dynamic_slice_in_dim(value_acc, offset, 3 * block_size, 0) + grad_values,
            offset,
            0,
        )
        query_acc = lax.dynamic_update_slice_in_dim(query_acc, grad_query, offset, 0)
        return (key_acc, value_acc, query_acc)

    start_state = (
        jnp.zeros(acc_shape, jnp.float32),
        jnp.zeros(acc_shape, jnp.float32),
        jnp.zeros(query_heads.shape, jnp.float32),
    )
    key_acc, value_acc, query_acc = lax.fori_loop(
        0, row_count // block_size, one_block, start_state
    )
    key_grad = key_acc[block_size : block_size + row_count].astype(jnp.bfloat16)
    value_grad = value_acc[block_size : block_size + row_count].astype(jnp.bfloat16)
    return (query_acc.astype(jnp.bfloat16), key_grad, value_grad)


def spread(vector):
    parts = lax.axis_size("tensor")
    length = vector.shape[-1]
    full = jnp.zeros(vector.shape[:-1] + (length * parts,), jnp.float32)
    return lax.dynamic_update_slice_in_dim(
        full, vector, lax.axis_index("tensor") * length, vector.ndim - 1
    )


def shards(
    tokens,
    segment_ids,
    out_grad,
    w_qkv,
    b_qv,
    w_out,
    b_out,
    norm1_gain,
    norm1_bias,
    w_up,
    b_up,
    w_down,
    b_down,
    norm2_gain,
    norm2_bias,
):
    full_qkv, full_out, full_up, full_down = (
        lax.all_gather(w_qkv, "dp", axis=0, tiled=True),
        lax.all_gather(w_out, "dp", axis=1, tiled=True),
        lax.all_gather(w_up, "dp", axis=0, tiled=True),
        lax.all_gather(w_down, "dp", axis=1, tiled=True),
    )
    model_width = full_qkv.shape[0]
    columns = full_qkv.shape[2]
    gathered = lax.all_gather(tokens, "tensor", axis=0, tiled=True)
    row_count = gathered.shape[0]
    segments = segment_ids[0]
    flat_qkv = full_qkv.reshape(model_width, 3 * columns)
    projected = jnp.dot(gathered, flat_qkv, preferred_element_type=jnp.float32).reshape(
        row_count, 3, columns
    )
    bias_qv = b_qv.astype(jnp.float32)
    head_shape = (row_count, columns // HD, HD)
    query_heads = (projected[:, 0] + bias_qv[0]).astype(jnp.bfloat16).reshape(head_shape)
    key_heads = projected[:, 1].astype(jnp.bfloat16).reshape(head_shape)
    value_heads = (projected[:, 2] + bias_qv[1]).astype(jnp.bfloat16).reshape(head_shape)
    context, log_totals = attention_forward(query_heads, key_heads, value_heads, segments)
    context = context.reshape(row_count, columns)
    attention = lax.psum_scatter(
        jnp.dot(context, full_out, preferred_element_type=jnp.float32).astype(jnp.bfloat16),
        "tensor",
        scatter_dimension=0,
        tiled=True,
    ).astype(jnp.float32) + b_out.astype(jnp.float32)
    gain_one = norm1_gain.astype(jnp.float32)
    gain_two = norm2_gain.astype(jnp.float32)
    hidden1, normed1, inverse1 = norm_forward(
        tokens.astype(jnp.float32) + attention, gain_one, norm1_bias.astype(jnp.float32)
    )
    hidden_low = hidden1.astype(jnp.bfloat16)
    mid_rows = lax.all_gather(hidden_low, "tensor", axis=0, tiled=True)
    hidden_pre = jnp.dot(mid_rows, full_up, preferred_element_type=jnp.float32) + b_up.astype(
        jnp.float32
    )
    activated = jax.nn.gelu(hidden_pre, approximate=False).astype(jnp.bfloat16)
    feed_out = lax.psum_scatter(
        jnp.dot(activated, full_down, preferred_element_type=jnp.float32).astype(jnp.bfloat16),
        "tensor",
        scatter_dimension=0,
        tiled=True,
    ).astype(jnp.float32) + b_down.astype(jnp.float32)
    output, normed2, inverse2 = norm_forward(
        hidden1 + feed_out, gain_two, norm2_bias.astype(jnp.float32)
    )
    grad_output = out_grad.astype(jnp.float32)
    grad_gain_two = jnp.sum(grad_output * normed2, axis=0)
    grad_bias_two = jnp.sum(grad_output, axis=0)
    grad_sum2 = norm_backward(grad_output, gain_two, normed2, inverse2)
    grad_feed = grad_sum2.astype(jnp.bfloat16)
    grad_b_down = jnp.sum(grad_feed, axis=0, dtype=jnp.float32)
    grad_mid_rows = lax.all_gather(grad_feed, "tensor", axis=0, tiled=True)
    grad_w_down = rows_product(activated, grad_mid_rows)
    grad_pre = (transposed(grad_mid_rows, full_down) * gelu_slope(hidden_pre)).astype(jnp.bfloat16)
    grad_w_up = rows_product(mid_rows, grad_pre)
    bias_up_full = spread(jnp.sum(grad_pre, axis=0, dtype=jnp.float32))
    grad_hidden1 = grad_sum2 + lax.psum_scatter(
        transposed(grad_pre, full_up).astype(jnp.bfloat16),
        "tensor",
        scatter_dimension=0,
        tiled=True,
    ).astype(jnp.float32)
    grad_gain_one = jnp.sum(grad_hidden1 * normed1, axis=0)
    grad_bias_one = jnp.sum(grad_hidden1, axis=0)
    grad_sum1 = norm_backward(grad_hidden1, gain_one, normed1, inverse1)
    grad_attn = grad_sum1.astype(jnp.bfloat16)
    grad_b_out = jnp.sum(grad_attn, axis=0, dtype=jnp.float32)
    grad_attn_rows = lax.all_gather(grad_attn, "tensor", axis=0, tiled=True)
    grad_w_out = rows_product(context, grad_attn_rows)
    grad_context = transposed(grad_attn_rows, full_out).astype(jnp.bfloat16).reshape(head_shape)
    grad_query, grad_keys, grad_values = attention_backward(
        query_heads, key_heads, value_heads, segments, log_totals, grad_context
    )
    grad_projected = jnp.stack([grad_query, grad_keys, grad_values], axis=1).reshape(
        row_count, 3 * columns
    )
    grad_w_qkv = rows_product(gathered, grad_projected).reshape(model_width, 3, columns)
    grad_tokens = grad_sum1 + lax.psum_scatter(
        transposed(grad_projected, flat_qkv).astype(jnp.bfloat16),
        "tensor",
        scatter_dimension=0,
        tiled=True,
    ).astype(jnp.float32)
    bias_qv_local = jnp.stack(
        [
            jnp.sum(grad_query, axis=0, dtype=jnp.float32).reshape(columns),
            jnp.sum(grad_values, axis=0, dtype=jnp.float32).reshape(columns),
        ],
        axis=0,
    )
    bias_qv_full = spread(bias_qv_local)
    out_qkv, out_wout, out_up, out_down = (
        lax.psum_scatter(
            grad_w_qkv.astype(jnp.bfloat16), "dp", scatter_dimension=0, tiled=True
        ).astype(jnp.float32),
        lax.psum_scatter(
            grad_w_out.astype(jnp.bfloat16), "dp", scatter_dimension=1, tiled=True
        ).astype(jnp.float32),
        lax.psum_scatter(
            grad_w_up.astype(jnp.bfloat16), "dp", scatter_dimension=0, tiled=True
        ).astype(jnp.float32),
        lax.psum_scatter(
            grad_w_down.astype(jnp.bfloat16), "dp", scatter_dimension=1, tiled=True
        ).astype(jnp.float32),
    )
    sum_qv, sum_up, sum_bout, sum_gain_one, sum_bias_one, sum_bdown, sum_gain_two, sum_bias_two = (
        lax.psum(
            (
                bias_qv_full,
                bias_up_full,
                grad_b_out,
                grad_gain_one,
                grad_bias_one,
                grad_b_down,
                grad_gain_two,
                grad_bias_two,
            ),
            ("dp", "tensor"),
        )
    )
    up_width = b_up.shape[0]
    out_bqv = lax.dynamic_slice_in_dim(sum_qv, lax.axis_index("tensor") * columns, columns, 1)
    out_bup = lax.dynamic_slice_in_dim(sum_up, lax.axis_index("tensor") * up_width, up_width, 0)
    return (
        output.astype(jnp.bfloat16),
        grad_tokens.astype(jnp.bfloat16),
        out_qkv,
        out_bqv,
        out_wout,
        sum_bout,
        sum_gain_one,
        sum_bias_one,
        out_up,
        out_bup,
        out_down,
        sum_bdown,
        sum_gain_two,
        sum_bias_two,
    )


def solution(mesh):
    in_specs = (
        P(("dp", "tensor"), None),
        P("dp", None),
        P(("dp", "tensor"), None),
        P("dp", None, "tensor"),
        P(None, "tensor"),
        P("tensor", "dp"),
        P(),
        P(),
        P(),
        P("dp", "tensor"),
        P("tensor"),
        P("tensor", "dp"),
        P(),
        P(),
        P(),
    )
    out_specs = (
        P(("dp", "tensor"), None),
        P(("dp", "tensor"), None),
        P("dp", None, "tensor"),
        P(None, "tensor"),
        P("tensor", "dp"),
        P(),
        P(),
        P(),
        P("dp", "tensor"),
        P("tensor"),
        P("tensor", "dp"),
        P(),
        P(),
        P(),
    )
    return jax.shard_map(shards, mesh=mesh, in_specs=in_specs, out_specs=out_specs, check_vma=False)
```

profile of v0, /device:TPU:0, one launch (start us, length us, event | category | flops | bytes accessed | tf_op | source)
XLA Modules:
  0.0 700.0 jit_solution(6280235299523345432)
XLA Ops:
  11.4 13.5 %all_gather.26 = bf16[256,1024]{1,0:T(8,128)(2,1)} all-gather(bf16[256,128]{1,0:T(8,128)(2,1)} %param.24), channel_id=1, replica_groups=mesh['dp'=8,'tensor'=4] {'dp'}, dimensions={1}, use_global_device_ids=true | all-gather | bytes 589824 | tf_op jit(solution)/shard_map/all_gather | solution.py:183
  24.8 14.4 %all-gather.10.cloned.1.call-done = bf16[1024,3,256]{0,2,1:T(8,128)(2,1)} async-done(((bf16[128,3,256]{0,2,1:T(8,128)(2,1)}), bf16[1024,3,256]{0,2,1:T(8,128)(2,1)}) %all-gather.10.cloned.1.call-update) | async-done | bytes 1572880 | tf_op jit(solution)/shard_map/all_gather | solution.py:182
  39.3 47.3 %all-gather.8.cloned.1.call-done = bf16[1024,1024]{1,0:T(8,128)(2,1)} async-done(((bf16[256,1024]{1,0:T(8,128)(2,1)}), bf16[1024,1024]{1,0:T(8,128)(2,1)}) %all-gather.8.cloned.1.call-update) | async-done | bytes 2097168 | tf_op jit(solution)/shard_map/all_gather | solution.py:189
  91.4 25.5 %while.29 = (s32[]{:T(128)}, bf16[2,512,4,64]{1,3,2,0:T(8,128)(2,1)}, f32[2,4,512]{2,1,0:T(4,128)S(1)}, s32[2]{0:T(128)S(1)}, bf16[2048,4,64]{0,2,1:T(8,128)(2,1...) while((s32[]{:T(128)}, ...), condition=%wide.region_3.4_spmd, body=%wide.region_0.3_spmd.sunk | while | flops 843970560 | bytes 47276340 | solution.py:84
  123.3 41.9 %reduce-scatter.13.cloned.1.call-done = bf16[256,1024]{1,0:T(8,128)(2,1)} async-done(((bf16[1024,1024]{1,0:T(8,128)(2,1)}), bf16[256,1024]{1,0:T(8,128)(2,1)}) %reduce-scatter.13.cloned.1.call-update) | async-done | bytes 524304 | tf_op jit(solution)/shard_map/reduce_scatter | solution.py:203
  171.0 22.9 %all-gather.14.cloned.1.call-done = bf16[1024,1024]{1,0:T(8,128)(2,1)} async-done(((bf16[128,1024]{1,0:T(8,128)(2,1)}), bf16[1024,1024]{1,0:T(8,128)(2,1)}) %all-gather.14.cloned.1.call-update) | async-done | bytes 2097168 | tf_op jit(solution)/shard_map/all_gather | solution.py:184
  193.9 47.7 %all-gather.12.cloned.1.call-done = bf16[1024,1024]{1,0:T(8,128)(2,1)} async-done(((bf16[256,1024]{1,0:T(8,128)(2,1)}), bf16[1024,1024]{1,0:T(8,128)(2,1)}) %all-gather.12.cloned.1.call-update) | async-done | bytes 2097168 | tf_op jit(solution)/shard_map/all_gather | solution.py:215
  241.6 14.5 %fusion.45 = (bf16[1024,1024]{1,0:T(8,128)(2,1)}, f32[1024,1024]{1,0:T(8,128)}) fusion(f32[1024]{0:T(1024)S(1)} %convert_element_type.180, bf16[1024,1024]{1,0:T(8,128)(2,1)} %all-gather.12.cloned.1.call-done, bf16[1024,1024]{1,0:T(8,128)(2,1)} %all-gather.14.cloned.1.call-done), kind=kOutput, calls=%fused_computation.53 | convolution fusion | flops 2216689664 | bytes 10489856 | tf_op jit(solution)/shard_map/dot_general | solution.py:216
  256.1 14.2 %all-gather.16.cloned.1.call-done = bf16[1024,1024]{1,0:T(8,128)(2,1)} async-done(((bf16[1024,128]{1,0:T(8,128)(2,1)}), bf16[1024,1024]{1,0:T(8,128)(2,1)}) %all-gather.16.cloned.1.call-update) | async-done | bytes 2097168 | tf_op jit(solution)/shard_map/all_gather | solution.py:185
  270.3 5.9 convolution_convert_fusion.3
  276.3 43.7 %reduce-scatter.15.cloned.1.call-done = bf16[256,1024]{1,0:T(8,128)(2,1)} async-done(((bf16[1024,1024]{1,0:T(8,128)(2,1)}), bf16[256,1024]{1,0:T(8,128)(2,1)}) %reduce-scatter.15.cloned.1.call-update) | async-done | bytes 524304 | tf_op jit(solution)/shard_map/reduce_scatter | solution.py:220
  326.7 45.0 %all-gather.18.cloned.1.call-done = bf16[1024,1024]{1,0:T(8,128)(2,1)} async-done(((bf16[256,1024]{1,0:T(8,128)(2,1)}), bf16[1024,1024]{1,0:T(8,128)(2,1)}) %all-gather.18.cloned.1.call-update) | async-done | bytes 2097168 | tf_op jit(solution)/shard_map/all_gather | solution.py:235
  371.7 7.2 %convert_reduce_fusion = (f32[1024]{0:T(1024)}, bf16[1024,1024]{1,0:T(8,128)(2,1)S(1)}) fusion(f32[1024,1024]{1,0:T(8,128)} %get-tuple-element.327, f32[1024]{0:T(1024)S(1)} %convert_element_type.180, bf16[1024,1024]{1,0:T(8,128)(2,1)} %all-gather.18.cloned.1.call-done, bf16[1024,1024]{1,0:T(8,128)(2,1)} %all-gather.16.cloned.1.call-done), kind=kOutput, calls=%fused_computation.60 | convolution fusion | flops 2161114112 | bytes 10493952 | tf_op jit(solution)/shard_map/dot_general | solution.py:18
  384.0 42.5 %reduce-scatter.17.cloned.1.call-done = bf16[256,1024]{1,0:T(8,128)(2,1)} async-done(((bf16[1024,1024]{1,0:T(8,128)(2,1)}), bf16[256,1024]{1,0:T(8,128)(2,1)}) %reduce-scatter.17.cloned.1.call-update) | async-done | bytes 524304 | tf_op jit(solution)/shard_map/reduce_scatter | solution.py:240
  433.2 5.9 convolution_convert_fusion
  443.2 5.9 convolution_convert_fusion.1
  449.3 28.8 %all-gather.20.cloned.1.call-done = bf16[1024,1024]{1,0:T(8,128)(2,1)} async-done(((bf16[256,1024]{1,0:T(8,128)(2,1)}), bf16[1024,1024]{1,0:T(8,128)(2,1)}) %all-gather.20.cloned.1.call-update) | async-done | bytes 2097168 | tf_op jit(solution)/shard_map/all_gather | solution.py:251
  484.6 48.4 %while.30 = (s32[]{:T(128)}, f32[2048,4,64]{0,2,1:T(8,128)}, f32[2048,4,64]{0,2,1:T(8,128)}, bf16[1024,4,64]{0,2,1:T(8,128)(2,1)}, bf16[1024,4,64]{0,2,1:T(8,128...) while((s32[]{:T(128)}, f32[2048,4,64]{0,2,1:T(8,128)}, ...), condition=%wide.region_17.18_spmd, body=%wide.region_15.17_spmd.sunk | while | flops 2043672576 | bytes 156566032 | solution.py:147
  488.2 5.7 multiply_reduce_fusion.7
  512.3 5.7 multiply_reduce_fusion.7
  553.6 12.1 %reduce-scatter.23.cloned.1.call-done = bf16[128,1024]{1,0:T(8,128)(2,1)} async-done(((bf16[1024,1024]{1,0:T(8,128)(2,1)}), bf16[128,1024]{1,0:T(8,128)(2,1)}) %reduce-scatter.23.cloned.1.call-update) | async-done | bytes 262160 | tf_op jit(solution)/shard_map/reduce_scatter | solution.py:282
  568.1 40.7 %all-reduce.3 = (f32[2,1024]{1,0:T(2,128)S(1)}, f32[1024]{0:T(1024)}, f32[1024]{0:T(1024)}, f32[1024]{0:T(1024)}, f32[4096]{0:T(1024)S(1)}, /*index=5*/f32[1024]{0:T(1024)}, f32[1024]{0:T(1024)}, f32[1024]{0:T(1024)}) all-reduce(f32[2,1024]{1,0:T(2,128)S(1)} %maximum_dynamic-update-slice_fusio, ...), channel_id=1, replica_groups=mesh['dp'=8,'tensor'=4] {'dp','tensor'}, use_global_device_ids=true, to_apply=%region_22.23 | all-reduce | flops 12288 | bytes 98304 | tf_op jit(solution)/shard_map/psum | solution.py:290
  611.6 33.5 %reduce-scatter.21.cloned.1.call-done = bf16[128,3,256]{2,0,1:T(8,128)(2,1)} async-done(((bf16[1024,3,256]{2,0,1:T(8,128)(2,1)}), bf16[128,3,256]{2,0,1:T(8,128)(2,1)}) %reduce-scatter.21.cloned.1.call-update) | async-done | bytes 196624 | tf_op jit(solution)/shard_map/reduce_scatter | solution.py:276
  646.9 44.1 %reduce-scatter.19.cloned.1.call-done = bf16[256,1024]{1,0:T(8,128)(2,1)} async-done(((bf16[1024,1024]{1,0:T(8,128)(2,1)}), bf16[256,1024]{1,0:T(8,128)(2,1)}) %reduce-scatter.19.cloned.1.call-update) | async-done | bytes 524304 | tf_op jit(solution)/shard_map/reduce_scatter | solution.py:261
  (231 shorter events, 140.6 us)
Async XLA Ops:
  7.2 32.1 %all-gather.10.cloned.1.call-start = ((), (), s32[]{:S(2)}) async-start(), calls=%async_computation.9 | async-start | bytes 1769472 | tf_op jit(solution)/shard_map/all_gather | solution.py:182
  9.0 77.5 %all-gather.8.cloned.1.call-start = ((), (), s32[]{:S(2)}) async-start(), calls=%async_computation.8 | async-start | bytes 2621440 | tf_op jit(solution)/shard_map/all_gather | solution.py:189
  9.7 155.4 %reduce-scatter.13.cloned.1.call-start = ((), (), s32[]{:S(2)}) async-start(), calls=%async_computation.10 | async-start | bytes 2621440 | tf_op jit(solution)/shard_map/reduce_scatter | solution.py:203
  116.9 48.3 %copy-start.4 = (bf16[256,1024]{1,0:T(8,128)(2,1)S(1)}, bf16[256,1024]{1,0:T(8,128)(2,1)}, u32[]{:S(2)}) copy-start(bf16[256,1024]{1,0:T(8,128)(2,1)} %param.19) | copy-start | bytes 1572868
  122.6 48.4 %copy-start.28 = (bf16[1024]{0:T(1024)(128)(2,1)S(1)}, bf16[1024]{0:T(1024)(128)(2,1)}, u32[]{:S(2)}) copy-start(bf16[1024]{0:T(1024)(128)(2,1)} %param.29) | copy-start | bytes 6148
  122.6 71.3 %all-gather.14.cloned.1.call-start = ((), (), s32[]{:S(2)}) async-start(), calls=%async_computation.12 | async-start | bytes 2359296 | tf_op jit(solution)/shard_map/all_gather | solution.py:184
  123.2 118.4 %all-gather.12.cloned.1.call-start = ((), (), s32[]{:S(2)}) async-start(), calls=%async_computation.11 | async-start | bytes 2621440 | tf_op jit(solution)/shard_map/all_gather | solution.py:215
  170.0 100.3 %all-gather.16.cloned.1.call-start = ((), (), s32[]{:S(2)}) async-start(), calls=%async_computation.13 | async-start | bytes 2359296 | tf_op jit(solution)/shard_map/all_gather | solution.py:185
  170.6 149.4 %reduce-scatter.15.cloned.1.call-start = ((), (), s32[]{:S(2)}) async-start(), calls=%async_computation.14 | async-start | bytes 2621440 | tf_op jit(solution)/shard_map/reduce_scatter | solution.py:220
  276.2 95.5 %all-gather.18.cloned.1.call-start = ((), (), s32[]{:S(2)}) async-start(), calls=%async_computation.15 | async-start | bytes 2621440 | tf_op jit(solution)/shard_map/all_gather | solution.py:235
  326.7 99.9 %reduce-scatter.17.cloned.1.call-start = ((), (), s32[]{:S(2)}) async-start(), calls=%async_computation.16 | async-start | bytes 2621440 | tf_op jit(solution)/shard_map/reduce_scatter | solution.py:240
  371.7 8.6 %copy-start.33 = (bf16[1024,1024]{1,0:T(8,128)(2,1)S(1)}, bf16[1024,1024]{1,0:T(8,128)(2,1)}, u32[]{:S(2)}) copy-start(bf16[1024,1024]{1,0:T(8,128)(2,1)} %all-gather.14.cloned.1.call-done) | copy-start | bytes 6291460
  384.0 94.2 %all-gather.20.cloned.1.call-start = ((), (), s32[]{:S(2)}) async-start(), calls=%async_computation.17 | async-start | bytes 2621440 | tf_op jit(solution)/shard_map/all_gather | solution.py:251
  433.1 118.5 %reduce-scatter.27.cloned.1.call-start = ((), (), s32[]{:S(2)}) async-start(), calls=%async_computation.22 | async-start | bytes 2359296
  443.1 122.6 %reduce-scatter.23.cloned.1.call-start = ((), (), s32[]{:S(2)}) async-start(), calls=%async_computation.20 | async-start | bytes 2359296 | tf_op jit(solution)/shard_map/reduce_scatter | solution.py:282
  449.1 160.9 %reduce-scatter.25.cloned.1.call-start = ((), (), s32[]{:S(2)}) async-start(), calls=%async_computation.21 | async-start | bytes 589824
  538.1 107.1 %reduce-scatter.21.cloned.1.call-start = ((), (), s32[]{:S(2)}) async-start(), calls=%async_computation.19 | async-start | bytes 1769472 | tf_op jit(solution)/shard_map/reduce_scatter | solution.py:276
  546.1 144.8 %reduce-scatter.19.cloned.1.call-start = ((), (), s32[]{:S(2)}) async-start(), calls=%async_computation.18 | async-start | bytes 2621440 | tf_op jit(solution)/shard_map/reduce_scatter | solution.py:261
  551.3 16.8 %copy-start.18 = (f32[1024]{0:T(1024)S(1)}, f32[1024]{0:T(1024)}, u32[]{:S(2)}) copy-start(f32[1024]{0:T(1024)} %get-tuple-element.256) | copy-start | bytes 12292
  551.3 16.8 %copy-start.19 = (f32[1024]{0:T(1024)S(1)}, f32[1024]{0:T(1024)}, u32[]{:S(2)}) copy-start(f32[1024]{0:T(1024)} %get-tuple-element.260) | copy-start | bytes 12292
  551.3 16.8 %copy-start.20 = (f32[1024]{0:T(1024)S(1)}, f32[1024]{0:T(1024)}, u32[]{:S(2)}) copy-start(f32[1024]{0:T(1024)} %get-tuple-element.311) | copy-start | bytes 12292
  551.3 16.8 %copy-start.21 = (f32[1024]{0:T(1024)S(1)}, f32[1024]{0:T(1024)}, u32[]{:S(2)}) copy-start(f32[1024]{0:T(1024)} %get-tuple-element.253) | copy-start | bytes 12292
  551.3 16.8 %copy-start.22 = (f32[1024]{0:T(1024)S(1)}, f32[1024]{0:T(1024)}, u32[]{:S(2)}) copy-start(f32[1024]{0:T(1024)} %get-tuple-element.258) | copy-start | bytes 12292
  551.3 16.8 %copy-start.23 = (f32[1024]{0:T(1024)S(1)}, f32[1024]{0:T(1024)}, u32[]{:S(2)}) copy-start(f32[1024]{0:T(1024)} %get-tuple-element.314) | copy-start | bytes 12292
  (37 other events, 135.4 us)
Sparse Core Ops, SparseCore 0:
  10.4 28.7 all-gather.9
  40.8 45.6 all-gather.7
  122.7 42.4 reduce-scatter.12
  166.9 26.9 all-gather.13
  195.9 45.6 all-gather.11
  243.3 26.8 all-gather.15
  276.3 43.6 reduce-scatter.14
  326.8 44.8 all-gather.17
  384.1 42.4 reduce-scatter.16
  433.3 44.8 all-gather.19
  481.4 39.9 reduce-scatter.26
  524.6 41.1 reduce-scatter.22
  569.4 34.0 reduce-scatter.24
  606.7 38.4 reduce-scatter.20
  647.3 43.6 reduce-scatter.18
where the time goes:
time: 709 us; the launch traced here: 700 us
  waiting for transfers between devices  440 us (62%)
  matrix products  114 us (16%)
  blocking collectives  54.2 us (8%)
  other arithmetic  45.3 us (6%)
  local copies, waits for them, and re-layouts  29.2 us (4%)
  between operations  14.7 us (2%)
    all_gather x1, waiting for transfers between devices, shards(): mid_rows = lax.all_gather(hidden_low, 'tensor', axis=0, tiled=True)  47.7 us
    all_gather x1, waiting for transfers between devices, shards(): gathered = lax.all_gather(tokens, 'tensor', axis=0, tiled=True)  47.3 us
    all_gather x1, waiting for transfers between devices, shards(): grad_mid_rows = lax.all_gather(grad_feed, 'tensor', axis=0, tiled=True)  45 us
    reduce_scatter x1, waiting for transfers between devices, shards(): lax.psum_scatter(transposed(grad_projected, flat_qkv).astype(jnp.bfloat16...  44.1 us
    reduce_scatter x1, waiting for transfers between devices, shards(): lax.psum_scatter(jnp.dot(activated, full_down, preferred_element_type=jnp...  43.7 us
    reduce_scatter x1, waiting for transfers between devices, shards(): lax.psum_scatter(transposed(grad_pre, full_up).astype(jnp.bfloat16), 'ten...  42.5 us
    reduce_scatter x1, waiting for transfers between devices, shards(): lax.psum_scatter(jnp.dot(context, full_out, preferred_element_type=jnp.fl...  41.9 us
    psum x1, blocking collectives, shards(): lax.psum((bias_qv_full, bias_up_full, grad_b_out, grad_gain_one, grad_bia...  40.7 us
  transfers between devices with their start and end apart: 15, of which 13 were waited for; matrix products, arithmetic and copies ran while one was open for 17% of the time, Pallas kernels for 0%

commit v1 on v0

v1 whole, which is shorter than its diff:
```python
import functools
import math
from types import SimpleNamespace

import jax
import jax.numpy as jnp
from jax import lax
from jax.experimental import pallas as pl
from jax.experimental.pallas import tpu as pltpu
from jax.sharding import PartitionSpec as P

HD = 64
MESH = pl.DeviceIdType.MESH
BF = jnp.bfloat16
F32 = jnp.float32
NEG = -1e30
VMEM_LIMIT = 67043328
MID, GF, FSND, FRCV = 0, 2, 4, 5


def nn(a, b):
    return jnp.dot(a, b, preferred_element_type=F32)


def nt(a, b):
    return lax.dot_general(a, b, (((1,), (1,)), ((), ())), preferred_element_type=F32)


def merge(x):
    return x.reshape(-1, x.shape[-1])


def spin(lo, hi, body):
    def step(i, carry):
        body(i)
        return carry

    lax.fori_loop(lo, hi, step, 0)


def order_table(T):
    return [sorted(range(T), key=lambda b: (abs(b - a), b if a < T / 2 else -b)) for a in range(T)]


def layer_kernel(cf, names, *refs):
    r = SimpleNamespace(**dict(zip(names, refs)))
    T, NQ, TB, D, R, C, HC, DP = cf.T, cf.NQ, cf.TB, cf.D, cf.R, cf.C, cf.HC, cf.DP
    S = NQ // 2
    RW = T * TB
    RC = 32
    heads = C // HD
    table = order_table(T)

    d = lax.axis_index("dp")
    t = lax.axis_index("tensor")
    q = lax.div(d, 2)
    c = d - 2 * q
    oc = 1 - c
    partner = (2 * q + oc, t)

    def perm(x):
        if NQ % 4:
            return x
        m = lax.rem(x, 4)
        return x + lax.div(m, 2) * (1 - 2 * lax.rem(m, 2))

    pos = perm(q)

    def chip_at(x):
        return perm(lax.rem(x + 4 * NQ, NQ))

    nxt = (2 * chip_at(pos + 1) + c, t)
    prv = (2 * chip_at(pos - 1) + c, t)

    def ind(a, b, n):
        x = lax.rem(a - b + n, n)
        return 1 - lax.div(x + n - 1, n)

    def tp(j):
        if isinstance(j, int):
            return sum(table[a][j] * ind(t, a, T) for a in range(T))
        js = [ind(j, b, T) for b in range(T)]
        total = 0
        for a in range(T):
            total = total + ind(t, a, T) * sum(table[a][b] * js[b] for b in range(T))
        return total

    def copy(src, dst, ss, rs, dev):
        return pltpu.make_async_remote_copy(
            src_ref=src, dst_ref=dst, send_sem=ss, recv_sem=rs, device_id=dev, device_id_type=MESH
        )

    def go(cp, op):
        if op == "start":
            cp.start()
        else:
            cp.wait_send()

    def half(kd, ref, h):
        if kd.split:
            return ref.at[h]
        n = kd.rows // 2
        return ref.at[pl.ds(h * n, n)]

    kt = SimpleNamespace(piece=lambda tt, qq: r.X.at[tt], zs=r.t_zs, zr=r.t_zr)
    kq = SimpleNamespace(
        piece=lambda tt, qq: r.Wq.at[2 * qq + c], split=False, rows=R, rs=r.q_rs, rr=r.q_rr,
        gs=r.q_gs, gr=r.q_gr, HB=r.q_HB, FB=r.q_FB,
    )
    ko = SimpleNamespace(
        piece=lambda tt, qq: r.Wo.at[tt, 2 * qq + c], split=False, rows=R, zs=r.o_zs, zr=r.o_zr,
        rs=r.o_rs, rr=r.o_rr, gs=r.o_gs, gr=r.o_gr, HB=r.o_HB, FB=r.o_FB,
        cs=r.o_cs, cr=r.o_cr, ZB=r.o_ZB,
    )
    ku = SimpleNamespace(
        piece=lambda tt, qq: r.Wu.at[tt, qq], split=True, rows=2 * R, zs=r.u_zs, zr=r.u_zr,
        rs=r.u_rs, rr=r.u_rr, gs=r.u_gs, gr=r.u_gr, HB=r.u_HB, FB=r.u_FB,
        cs=r.u_cs, cr=r.u_cr, ZB=r.u_ZB,
    )
    kd_ = SimpleNamespace(
        piece=lambda tt, qq: r.Wd.at[tt, qq], split=True, rows=2 * R, zs=r.d_zs, zr=r.d_zr,
        rs=r.d_rs, rr=r.d_rr, gs=r.d_gs, gr=r.d_gr, HB=r.d_HB, FB=r.d_FB,
        cs=r.d_cs, cr=r.d_cr, ZB=r.d_ZB,
    )
    kg = SimpleNamespace(piece=lambda tt, qq: r.POOL.at[tt], cs=r.g_cs, cr=r.g_cr, ZB=r.g_ZB)

    def z_right(k, tt, op):
        @pl.when((tt <= t) & (t < T - 1))
        def _():
            ref = k.piece(tt, q)
            go(copy(ref, ref, k.zs.at[tt, 0], k.zr.at[tt], (d, t + 1)), op)

    def z_left(k, tt, op):
        @pl.when((tt >= t) & (t > 0))
        def _():
            ref = k.piece(tt, q)
            go(copy(ref, ref, k.zs.at[tt, 1], k.zr.at[tt], (d, t - 1)), op)

    def z_send(k, tt, op="start"):
        z_right(k, tt, op)
        z_left(k, tt, op)

    def z_wait(k, tt):
        ref = k.piece(tt, q)
        copy(ref, ref, k.zs.at[tt, 0], k.zr.at[tt], partner).wait_recv()

    def ring_send(k, tt, s, op="start"):
        a = k.piece(tt, chip_at(pos - s))
        b = k.piece(tt, chip_at(pos + s))
        if s == S - 1:
            a, b = half(k, a, 0), half(k, b, 1)
        go(copy(a, a, k.rs.at[tt, 0, s], k.rr.at[tt, 0, s], nxt), op)
        go(copy(b, b, k.rs.at[tt, 1, s], k.rr.at[tt, 1, s], prv), op)

    def ring_wait(k, tt, s):
        a = k.piece(tt, chip_at(pos - 1 - s))
        b = k.piece(tt, chip_at(pos + 1 + s))
        if s == S - 1:
            a, b = half(k, a, 0), half(k, b, 1)
        copy(a, a, k.rs.at[tt, 0, s], k.rr.at[tt, 0, s], nxt).wait_recv()
        copy(b, b, k.rs.at[tt, 1, s], k.rr.at[tt, 1, s], prv).wait_recv()

    def twin_o(tt, qq):
        ref = r.Wo.at[tt, 2 * qq + c]
        copy(ref, ref, r.tw_s.at[0], r.tw_r.at[0], partner).start()

    def twin_q(tt, qq):
        ref = r.Wq.at[2 * qq + c]
        copy(ref, ref, r.tw_s.at[1], r.tw_r.at[1], partner).start()

    def arrived(k, tt, s, twin):
        ring_wait(k, tt, s)
        if twin is not None:
            twin(tt, chip_at(pos + 1 + s))
            if s < S - 1:
                twin(tt, chip_at(pos - 1 - s))

    def ring_adv(k, tt, twin=None):
        for s in range(1, S):
            arrived(k, tt, s - 1, twin)
            ring_send(k, tt, s)

    def ring_fin(k, tt, twin=None):
        arrived(k, tt, S - 1, twin)

    def add(dst, src):
        dst[...] = (dst[...].astype(F32) + src[...].astype(F32)).astype(BF)

    def rs_send(k, tt, s, op="start"):
        a = k.piece(tt, chip_at(pos + S - s))
        b = k.piece(tt, chip_at(pos - S + s))
        if s == 0:
            a, b = half(k, a, 0), half(k, b, 1)
            da, db = k.HB.at[tt, 0], k.HB.at[tt, 1]
        else:
            da, db = k.FB.at[tt, 0, s - 1], k.FB.at[tt, 1, s - 1]
        go(copy(a, da, k.gs.at[tt, 0, s], k.gr.at[tt, 0, s], nxt), op)
        go(copy(b, db, k.gs.at[tt, 1, s], k.gr.at[tt, 1, s], prv), op)

    def rs_add(k, tt, s):
        a = k.piece(tt, chip_at(pos + S - s - 1))
        b = k.piece(tt, chip_at(pos - S + s + 1))
        if s == 0:
            a, b = half(k, a, 0), half(k, b, 1)
            da, db = k.HB.at[tt, 0], k.HB.at[tt, 1]
        else:
            da, db = k.FB.at[tt, 0, s - 1], k.FB.at[tt, 1, s - 1]
        copy(da, da, k.gs.at[tt, 0, s], k.gr.at[tt, 0, s], nxt).wait_recv()
        add(a, da)
        copy(db, db, k.gs.at[tt, 1, s], k.gr.at[tt, 1, s], prv).wait_recv()
        add(b, db)

    def rs_mid(k, tt):
        for s in range(1, S):
            rs_add(k, tt, s - 1)
            rs_send(k, tt, s)

    def rs_last(k, tt):
        rs_add(k, tt, S - 1)

    def chain_send(k, tt, op="start"):
        ref = k.piece(tt, q)

        @pl.when(tt > t)
        def _():
            go(copy(ref, k.ZB.at[tt], k.cs.at[tt], k.cr.at[tt], (d, t + 1)), op)

        @pl.when(tt < t)
        def _():
            slot = tt + (T - tt) * ind(tt, t - 1, T)
            go(copy(ref, k.ZB.at[slot], k.cs.at[tt], k.cr.at[slot], (d, t - 1)), op)

    def chain_take(k, tt, slot):
        copy(k.ZB.at[slot], k.ZB.at[slot], k.cs.at[tt], k.cr.at[slot], partner).wait_recv()
        add(k.piece(tt, q), k.ZB.at[slot])

    def chain(k, tt):
        @pl.when(((tt >= t) & (t > 0)) | ((tt < t) & (t < T - 1)))
        def _():
            chain_take(k, tt, tt)

        @pl.when((tt == t) & (t < T - 1))
        def _():
            chain_take(k, tt, T)

        chain_send(k, tt)

    barrier = pltpu.get_barrier_semaphore()
    peers = [partner]
    peers += [(2 * lax.rem(q + k, NQ) + c, t) for k in range(1, NQ)]
    peers += [(d, lax.rem(t + k, T)) for k in range(1, T)]
    for peer in peers:
        pl.semaphore_signal(barrier, inc=1, device_id=peer, device_id_type=MESH)
    get_tok = pltpu.make_async_copy(r.tok, r.X.at[t], r.in_s.at[0])
    get_tok.start()
    get_og = pltpu.make_async_copy(r.og, r.out, r.in_s.at[1])
    get_og.start()
    r.Wq[d] = r.wq[...]
    r.Wo[t, d] = r.wo[...]
    lo = pl.multiple_of(c * HC, 128)
    r.Wu[t, q, c] = r.wu[:, pl.ds(lo, HC)]
    r.Wd[t, q, c] = r.wd[:, pl.ds(lo, HC)]
    ro = pl.multiple_of(oc * HC, 128)
    r.FSW[0] = r.wu[:, pl.ds(ro, HC)]
    r.FSW[1] = r.wd[:, pl.ds(ro, HC)]
    r.BU[t] = r.bup[c]
    get_tok.wait()
    get_og.wait()
    pl.semaphore_wait(barrier, len(peers))

    z_send(kt, t)
    z_send(ko, t)
    twin_q(0, q)
    ring_send(kq, 0, 0)
    swap_u = copy(r.FSW.at[0], r.Wu.at[t, q, c], r.sw_s.at[0], r.sw_r.at[0], partner)
    swap_d = copy(r.FSW.at[1], r.Wd.at[t, q, c], r.sw_s.at[1], r.sw_r.at[1], partner)
    swap_u.start()
    swap_d.start()
    twin_o(t, q)
    ring_send(ko, t, 0)
    for k in range(1, T):
        tt = lax.rem(t + k, T)
        copy(r.BU.at[t], r.BU.at[t], r.b_s.at[tt], r.b_r.at[t], (d, tt)).start()
    r.SACC[...] = jnp.zeros_like(r.SACC)
    r.SB[...] = jnp.zeros_like(r.SB)
    r.DK[...] = jnp.zeros_like(r.DK)
    r.DV[...] = jnp.zeros_like(r.DV)
    for n, (ref, w) in enumerate(((r.Wu, ku), (r.Wd, kd_))):
        copy(ref.at[t, q, oc], ref.at[t, q, oc], r.sw_s.at[n], r.sw_r.at[n], partner).wait_recv()
        ring_send(w, t, 0)

    def weights_z(tt):
        @pl.when(tt == 0)
        def _():
            z_right(ku, t, "start")

        @pl.when(tt == T - 1)
        def _():
            z_left(ku, t, "start")

    def project(tt):
        x = r.X[tt]
        at = pl.ds(pl.multiple_of(tt * TB, TB), TB)
        for part, name in enumerate(("Q", "K", "V")):
            w = merge(r.Wq[:, :, part * C : (part + 1) * C])
            y = nn(x, w) + r.bqkv[:, part * C : (part + 1) * C]
            y = y.astype(BF)
            if part == 0:
                r.Q[at, :] = y * jnp.asarray(HD ** (-0.5), BF)
            elif part == 1:
                r.K[at, :] = y
                r.KT[:, at] = y.astype(F32).T.astype(BF)
            else:
                r.V[at, :] = y
                r.VT[:, at] = y.astype(F32).T.astype(BF)

    weights_z(t)
    for s in range(S):
        arrived(kq, 0, s, twin_q)
        if s + 1 < S:
            ring_send(kq, 0, s + 1)
    copy(r.RQ, r.RQ, r.tw_s.at[1], r.tw_r.at[1], partner).wait_recv()
    project(t)
    for j in range(1, T):
        tt = tp(j)
        z_wait(kt, tt)
        z_send(kt, tt)
        z_wait(ko, tt)
        z_send(ko, tt)
        weights_z(tt)
        twin_o(tt, q)
        ring_send(ko, tt, 0)
        ring_adv(ko, tp(j - 1), twin_o)
        if j == 1:
            ring_adv(ku, t)
            ring_adv(kd_, t)
        else:
            ring_fin(ko, tp(j - 2), twin_o)
        project(tt)
    ring_adv(ko, tp(T - 1), twin_o)
    if T > 1:
        ring_fin(ko, tp(T - 2), twin_o)
    ring_fin(ko, tp(T - 1), twin_o)

    line = [(ku, j) for j in range(1, T)] + [(kd_, j) for j in range(1, T)]
    done = [0]

    def serve():
        n = done[0]
        done[0] += 1
        if n > len(line):
            return
        if n > 0:
            ring_adv(line[n - 1][0], tp(line[n - 1][1]))
        if n < len(line):
            k, j = line[n]
            tt = tp(j)
            z_wait(k, tt)
            z_send(k, tt)
            if n == 0:
                z_send(kd_, t)
            ring_send(k, tt, 0)

    lane = lax.broadcasted_iota(jnp.int32, (1, 128), 1)
    picks = [(lane < HD).astype(F32).astype(BF), (lane >= HD).astype(F32).astype(BF)]

    def bias_for(i):
        same = r.segc[:, 0:1] == r.segr[i]
        r.BIAS[...] = jnp.where(same, 0.0, NEG)

    def attend(j):
        i = lax.rem(t + 1 + j, T)
        at = pl.ds(pl.multiple_of(i * TB, TB), TB)
        bias_for(i)
        for h in range(heads):
            pair = slice((h // 2) * 128, (h // 2) * 128 + 128)
            qh = r.Q[at, pair] * picks[h % 2]
            sc = nt(r.K[:, pair], qh) + r.BIAS[...]
            top = jnp.max(sc, axis=0, keepdims=True)
            e = jnp.exp(sc - top)
            total = jnp.sum(e, axis=0, keepdims=True)
            ct = nn(r.VT[h * HD : (h + 1) * HD, :], e.astype(BF))
            r.CT[h * HD : (h + 1) * HD, :] = ct / total
            r.LSE[i, h : h + 1, :] = top + jnp.log(total)
        r.CXR[i] = r.CT[...].T.astype(BF)

        @pl.when(i != t)
        def _():
            copy(r.CXR.at[i], r.CTX.at[t], r.c_s.at[i], r.c_r.at[t], (d, i)).start()

    spin(0, T // 2, attend)
    serve()
    spin(T // 2, T, attend)
    serve()
    r.CTX[t] = r.CXR[t]
    for k in range(1, T):
        tt = lax.rem(t + k, T)
        copy(r.CTX.at[tt], r.CTX.at[tt], r.c_s.at[tt], r.c_r.at[tt], partner).wait_recv()
    copy(r.RWO, r.RWO, r.tw_s.at[0], r.tw_r.at[0], partner).wait_recv()

    def out_dot(j):
        y = nt(r.CTX[j], merge(r.Wo[j]))

        @pl.when(j == 0)
        def _():
            r.FEED[0] = y

        @pl.when(j > 0)
        def _():
            r.FEED[0] += y

    spin(0, T, out_dot)

    def rows_of(body):
        def step(i):
            body(pl.ds(pl.multiple_of(i * RC, RC), RC))

        spin(0, TB // RC, step)

    def tally(n, x):
        r.SACC[n] += x.reshape(RC // 8, 8, D).sum(axis=0)

    def norm(x):
        mid = x - jnp.mean(x, axis=-1, keepdims=True)
        inverse = lax.rsqrt(jnp.mean(mid * mid, axis=-1, keepdims=True) + 1e-05)
        return mid * inverse, inverse

    def norm_back(up, gain, normed, inverse):
        e = up * gain
        return inverse * (
            e - jnp.mean(e, axis=-1, keepdims=True) - normed * jnp.mean(e * normed, axis=-1, keepdims=True)
        )

    def vec(n):
        return r.vecs[n : n + 1, :]

    def first_norm(at):
        x = r.X[t, at, :].astype(F32) + r.FEED[0, at, :] + vec(0)
        normed, inverse = norm(x)
        h1 = normed * vec(1) + vec(2)
        r.N1[at, :] = normed
        r.IV1[at, :] = inverse
        r.H1[at, :] = h1
        r.POOL[MID + c, at, :] = h1.astype(BF)

    rows_of(first_norm)

    def exchange(n, base, op="start"):
        ref = r.POOL.at[base + c]
        go(copy(ref, ref, r.e_s.at[n], r.e_r.at[n], partner), op)

    def exchanged(n, base):
        ref = r.POOL.at[base + oc]
        copy(ref, ref, r.e_s.at[n], r.e_r.at[n], partner).wait_recv()

    exchange(0, MID)
    for k in range(1, T):
        tt = lax.rem(t + k, T)
        copy(r.BU.at[tt], r.BU.at[tt], r.b_s.at[tt], r.b_r.at[tt], partner).wait_recv()
    exchanged(0, MID)

    def turn(src, dst):
        def step(b):
            y = r.POOL[src + b].astype(F32).T.astype(BF)
            dst[:, pl.ds(pl.multiple_of(b * TB, TB), TB)] = y

        spin(0, 2, step)

    def up(j):
        tt = tp(j)
        ring_fin(ku, tt)
        w = merge(r.Wu[tt])
        bias = r.BU[tt]

        def block(b):
            r.PRE[...] = nn(r.POOL[MID + b], w) + bias

            def piece(i):
                at = pl.ds(pl.multiple_of(i * RC, RC), RC)
                v = r.PRE[at, :]
                cdf = 0.5 * (1.0 + lax.erf(v * 2.0 ** (-0.5)))
                slope = cdf + v * jnp.exp(-0.5 * v * v) * (2.0 * math.pi) ** (-0.5)
                to = pl.ds(pl.multiple_of(b * TB + i * RC, RC), RC)
                r.ACT[tt, to, :] = (v * cdf).astype(BF)
                r.SL[tt, to, :] = slope.astype(BF)

            spin(0, TB // RC, piece)

        spin(0, 2, block)

    up(0)
    for j in range(1, T):
        serve()
        up(j)
    turn(MID, r.MIDT)

    def down(j):
        tt = tp(j)
        ring_fin(kd_, tt)
        w = merge(r.Wd[tt])

        def block(b):
            y = nt(r.ACT[tt, pl.ds(pl.multiple_of(b * TB, TB), TB), :], w)
            if j == 0:
                r.FEED[b] = y
            else:
                r.FEED[b] += y

        spin(0, 2, block)

    for j in range(T):
        serve()
        down(j)
    while done[0] <= len(line):
        serve()

    def give(n):
        def step(at):
            r.POOL[FSND, at, :] = r.FEED[oc, at, :].astype(BF)

        rows_of(step)
        copy(r.POOL.at[FSND], r.POOL.at[FRCV], r.e_s.at[n], r.e_r.at[n], partner).start()
        copy(r.POOL.at[FRCV], r.POOL.at[FRCV], r.e_s.at[n], r.e_r.at[n], partner).wait_recv()
        copy(r.POOL.at[FSND], r.POOL.at[FRCV], r.e_s.at[n], r.e_r.at[n], partner).wait_send()

    def given(n, at):
        return r.FEED[c, at, :] + r.POOL[FRCV, at, :].astype(F32)

    give(1)

    def second_norm(at):
        x = r.H1[at, :] + given(1, at) + vec(3)
        normed, inverse = norm(x)
        g = r.out[at, :].astype(F32)
        r.out[at, :] = (normed * vec(4) + vec(5)).astype(BF)
        tally(0, g * normed)
        tally(1, g)
        back = norm_back(g, vec(4), normed, inverse)
        r.H1[at, :] = back
        low = back.astype(BF)
        r.POOL[GF + c, at, :] = low
        tally(2, low.astype(F32))

    rows_of(second_norm)
    exchange(2, GF)

    def drain_gather(k):
        def step(tt):
            if hasattr(k, "zs"):
                z_send(k, tt, "drain")
            for s in range(S):
                ring_send(k, tt, s, "drain")

        spin(0, T, step)

    drain_gather(ku)
    drain_gather(kd_)
    swap_u.wait_send()
    swap_d.wait_send()
    exchanged(2, GF)
    turn(GF, r.GFT)

    def slot_back(k):
        tt = tp(T - 1 - k)

        def block(b):
            to = pl.ds(pl.multiple_of(b * TB, TB), TB)
            r.PRE[...] = nn(r.POOL[GF + b], merge(r.Wd[tt]))

            def piece(i):
                at = pl.ds(pl.multiple_of(i * RC, RC), RC)
                tr = pl.ds(pl.multiple_of(b * TB + i * RC, RC), RC)
                gp = (r.PRE[at, :] * r.SL[tt, tr, :].astype(F32)).astype(BF)
                r.SL[tt, tr, :] = gp
                r.SBA[...] += gp.astype(F32).reshape(RC // 8, 8, HC).sum(axis=0)

            spin(0, TB // RC, piece)
            y = nt(r.SL[tt, to, :], merge(r.Wu[tt]))

            @pl.when(k == 0)
            def _():
                r.FEED[b] = y

            @pl.when(k > 0)
            def _():
                r.FEED[b] += y

        r.SBA[...] = jnp.zeros_like(r.SBA)
        spin(0, 2, block)
        r.SB[pl.ds(2 * tt + c, 1)] = r.SBA[...].sum(axis=0, keepdims=True)[None]

        def weight(qq):
            at = pl.ds(pl.multiple_of(qq * 2 * R, 2 * R), 2 * R)
            y = nn(r.GFT[at, :], r.ACT[tt])
            r.Wd[tt, qq] = y.astype(BF).reshape(2, R, HC)
            y = nn(r.MIDT[at, :], r.SL[tt])
            r.Wu[tt, qq] = y.astype(BF).reshape(2, R, HC)

        spin(0, NQ, weight)
        rs_send(kd_, tt, 0)
        rs_send(ku, tt, 0)

    spin(0, T, slot_back)
    give(3)

    def first_back(at):
        g = r.H1[at, :] + given(3, at)
        normed = r.N1[at, :]
        tally(3, g * normed)
        tally(4, g)
        back = norm_back(g, vec(1), normed, r.IV1[at, :])
        r.H1[at, :] = back
        low = back.astype(BF)
        r.gtok[at, :] = low
        tally(5, low.astype(F32))

    rows_of(first_back)

    def context_back(k):
        tt = tp(T - 1 - k)
        r.CXR[tt] = nn(r.gtok[...], merge(r.Wo[tt])).astype(BF)

        @pl.when(tt != t)
        def _():
            copy(r.CXR.at[tt], r.GC.at[t], r.gc_s.at[tt], r.gc_r.at[t], (d, tt)).start()

        @pl.when(tt == t)
        def _():
            r.GC[t] = r.CXR[t]

    for k in range(1, T):
        tt = lax.rem(t + k, T)
        copy(r.CXR.at[tt], r.CTX.at[t], r.c_s.at[tt], r.c_r.at[t], (d, tt)).wait_send()
    spin(0, T, context_back)
    drain_gather(ko)
    copy(r.RWO, r.RWO, r.tw_s.at[0], r.tw_r.at[0], partner).wait_send()

    r.GFT[:, 0:TB] = r.gtok[...].astype(F32).T.astype(BF)

    def out_back(tt):
        def weight(qq):
            at = pl.ds(pl.multiple_of(qq * 2 * R, 2 * R), 2 * R)
            y = nn(r.GFT[at, 0:TB], r.CTX[tt]).astype(BF)
            r.Wo[tt, pl.ds(2 * qq, 2)] = y.reshape(2, R, C)
            copy(r.Wo.at[tt, 2 * qq + oc], r.RWO.at[tt, qq], r.go_s.at[0], r.go_r.at[0], partner).start()

        spin(0, NQ, weight)

    spin(0, T, out_back)

    for n in range(6):
        r.SV[n : n + 1, :] = r.SACC[n].sum(axis=0, keepdims=True)
    r.SV[6:8, :] = jnp.zeros((2, D), F32)

    def sum_core(n, ref, box, op):
        cp = copy(ref, box, r.a_s.at[0, n], r.a_r.at[0, n], partner)
        if op == "start":
            cp.start()
        else:
            copy(box, box, r.a_s.at[0, n], r.a_r.at[0, n], partner).wait_recv()
            cp.wait_send()
            ref[...] += box[...]

    def sum_group(stage, n, ref, box, me, count, dev, op):
        if op == "start":
            box[me] = ref[...]
        for k in range(1, count):
            other = lax.rem(me + k, count)
            sems = r.ag_s.at[stage, n, other], r.ag_r.at[stage, n, me]
            if op == "start":
                copy(box.at[me], box.at[me], *sems, dev(other)).start()
            else:
                copy(box.at[me], box.at[me], *sems, dev(other)).wait_send()
                copy(
                    box.at[other], box.at[other], r.ag_s.at[stage, n, other],
                    r.ag_r.at[stage, n, other], dev(other),
                ).wait_recv()
        if op != "start":
            total = box[0]
            for k in range(1, count):
                total = total + box[k]
            ref[...] = total

    def chip_dev(other):
        return (2 * other + c, t)

    def row_dev(other):
        return (d, other)

    sum_core(0, r.SV, r.SV1, "start")
    sum_core(1, r.SB, r.SB1, "start")

    copy(r.RWO, r.RWO, r.go_s.at[0], r.go_r.at[0], partner).wait_recv()

    def out_join(k):
        tt = tp(T - 1 - k)

        def step(qq):
            add(r.Wo.at[tt, 2 * qq + c], r.RWO.at[tt, qq])

        spin(0, NQ, step)
        rs_send(ko, tt, 0)

    spin(0, T, out_join)
    sum_core(0, r.SV, r.SV1, "end")
    sum_core(1, r.SB, r.SB1, "end")
    sum_group(0, 0, r.SV, r.SV2, q, NQ, chip_dev, "start")
    sum_group(0, 1, r.SB, r.SB2, q, NQ, chip_dev, "start")

    def attend_back(j):
        i = tp(j)
        at = pl.ds(pl.multiple_of(i * TB, TB), TB)

        @pl.when(i != t)
        def _():
            copy(r.GC.at[i], r.GC.at[i], r.gc_s.at[i], r.gc_r.at[i], partner).wait_recv()

        bias_for(i)
        for h in range(heads):
            pair = slice((h // 2) * 128, (h // 2) * 128 + 128)
            qh = r.Q[at, pair] * picks[h % 2]
            gh = r.GC[i, :, pair] * picks[h % 2]
            pr = jnp.exp(nt(r.K[:, pair], qh) + r.BIAS[...] - r.LSE[i, h : h + 1, :])
            gp = nt(r.V[:, pair], gh)
            r.DV[:, pair] += nn(pr.astype(BF), gh)
            prod = pr * gp
            delta = jnp.sum(prod, axis=0, keepdims=True)
            ds = (prod - pr * delta).astype(BF)
            r.DK[:, pair] += nn(ds, qh)
            r.CT[h * HD : (h + 1) * HD, :] = nn(r.KT[h * HD : (h + 1) * HD, :], ds) * HD ** (-0.5)
        r.DPJ[i, :, 0:C] = r.CT[...].T.astype(BF)
        tt = tp(T - 1 - j)
        rs_mid(kd_, tt)
        rs_mid(ku, tt)
        rs_mid(ko, tt)

    spin(0, T, attend_back)
    sum_group(0, 0, r.SV, r.SV2, q, NQ, chip_dev, "end")
    sum_group(0, 1, r.SB, r.SB2, q, NQ, chip_dev, "end")
    sum_group(1, 0, r.SV, r.SV3, t, T, row_dev, "start")
    sum_group(1, 1, r.SB, r.SB3, t, T, row_dev, "start")

    exchange(0, MID, "drain")
    exchange(2, GF, "drain")

    r.SQ[...] = jnp.zeros_like(r.SQ)

    def input_back(k):
        tt = tp(T - 1 - k)
        at = pl.ds(pl.multiple_of(tt * TB, TB), TB)
        r.DPJ[tt, :, C : 2 * C] = r.DK[at, :].astype(BF)
        r.DPJ[tt, :, 2 * C : 3 * C] = r.DV[at, :].astype(BF)
        r.SQ[0:1, :] += r.DPJ[tt, :, 0:C].astype(F32).sum(axis=0, keepdims=True)
        r.SQ[1:2, :] += r.DPJ[tt, :, 2 * C : 3 * C].astype(F32).sum(axis=0, keepdims=True)
        r.POOL[tt] = nt(r.DPJ[tt], merge(r.Wq[...])).astype(BF)

        @pl.when(tt != t)
        def _():
            chain(kg, tt)

    spin(0, T, input_back)

    def settle(k, tt):
        rs_last(k, tt)

        @pl.when(tt != t)
        def _():
            chain(k, tt)

    sum_core(2, r.SQ, r.SQ1, "start")
    settle(kd_, tp(T - 1))
    settle(ku, tp(T - 1))

    copy(r.RQ, r.RQ, r.tw_s.at[1], r.tw_r.at[1], partner).wait_send()
    for s in range(S):
        ring_send(kq, 0, s, "drain")

    many = max(2, 256 // R)

    def qkv_weight(g):
        cols = pl.ds(pl.multiple_of(g * many * R, 128), many * R)
        x = merge(r.X[:, :, cols])
        y = lax.dot_general(
            x, merge(r.DPJ[...]), (((0,), (0,)), ((), ())), preferred_element_type=F32
        )
        r.Wq[pl.ds(many * g, many)] = y.astype(BF).reshape(many, R, 3 * C)
        for k in range(many // 2):
            qq = g * (many // 2) + k
            copy(r.Wq.at[2 * qq + oc], r.RQ.at[qq], r.go_s.at[1], r.go_r.at[1], partner).start()

    spin(0, DP // many, qkv_weight)
    sum_core(2, r.SQ, r.SQ1, "end")
    sum_group(0, 2, r.SQ, r.SQ2, q, NQ, chip_dev, "start")
    copy(r.RQ, r.RQ, r.go_s.at[1], r.go_r.at[1], partner).wait_recv()

    def q_join(qq):
        add(r.Wq.at[2 * qq + c], r.RQ.at[qq])

    spin(0, NQ, q_join)
    rs_send(kq, 0, 0)
    settle(ko, tp(T - 1))
    for j in range(T - 2, 0, -1):
        settle(kd_, tp(j))
        settle(ku, tp(j))
        settle(ko, tp(j))
        if j == T - 2:
            rs_mid(kq, 0)
    rs_last(kd_, t)
    rs_last(ku, t)
    rs_last(ko, t)
    rs_last(kq, 0)
    sum_group(1, 0, r.SV, r.SV3, t, T, row_dev, "end")
    sum_group(1, 1, r.SB, r.SB3, t, T, row_dev, "end")
    sum_group(0, 2, r.SQ, r.SQ2, q, NQ, chip_dev, "end")
    chain(kg, t)

    def finish(at):
        r.gtok[at, :] = (r.H1[at, :] + r.POOL[t, at, :].astype(F32)).astype(BF)

    rows_of(finish)
    chain(kd_, t)
    chain(ku, t)
    chain(ko, t)
    cps = []
    for n, ref in enumerate((r.Wu, r.Wd)):
        cp = copy(ref.at[t, q, oc], r.FSW.at[n], r.fs_s.at[n], r.fs_r.at[n], partner)
        cp.start()
        cps.append(cp)
    r.gwq[...] = r.Wq[d].astype(F32)
    r.gwo[...] = r.Wo[t, d].astype(F32)
    r.sv[...] = r.SV[...]
    r.sbq[...] = r.SQ[...]
    r.sbu[...] = r.SB[pl.ds(2 * t, 2)]
    for n, (ref, o) in enumerate(((r.Wu, r.gwu), (r.Wd, r.gwd))):
        copy(r.FSW.at[n], r.FSW.at[n], r.fs_s.at[n], r.fs_r.at[n], partner).wait_recv()
        o[:, pl.ds(lo, HC)] = ref[t, q, c].astype(F32)
        o[:, pl.ds(ro, HC)] = r.FSW[n].astype(F32)
        cps[n].wait_send()

    def drain(tt):
        z_send(kt, tt, "drain")
        for k in (kd_, ku, ko):
            for s in range(S):
                rs_send(k, tt, s, "drain")
            chain_send(k, tt, "drain")
        chain_send(kg, tt, "drain")

        @pl.when(tt != t)
        def _():
            copy(r.CXR.at[tt], r.GC.at[t], r.gc_s.at[tt], r.gc_r.at[t], (d, tt)).wait_send()
            copy(r.BU.at[t], r.BU.at[t], r.b_s.at[tt], r.b_r.at[t], (d, tt)).wait_send()

    spin(0, T, drain)
    for s in range(S):
        rs_send(kq, 0, s, "drain")
    copy(r.RWO, r.RWO, r.go_s.at[0], r.go_r.at[0], partner).wait_send()
    copy(r.RQ, r.RQ, r.go_s.at[1], r.go_r.at[1], partner).wait_send()


def layer(cf, *args):
    T, NQ, TB, D, R, C, HC, DP = cf.T, cf.NQ, cf.TB, cf.D, cf.R, cf.C, cf.HC, cf.DP
    S = NQ // 2
    RW = T * TB
    Cq = 3 * C
    heads = C // HD
    hp = -(-heads // 8) * 8
    dma = pltpu.SemaphoreType.DMA
    V = pltpu.VMEM
    ins = ["tok", "og", "wq", "wo", "wu", "wd", "bqkv", "bup", "vecs", "segc", "segr"]
    outs = {
        "out": ((TB, D), BF), "gtok": ((TB, D), BF), "gwq": ((R, Cq), F32), "gwo": ((R, C), F32),
        "gwu": ((R, 2 * HC), F32), "gwd": ((R, 2 * HC), F32), "sv": ((8, D), F32),
        "sbq": ((8, C), F32), "sbu": ((2, 1, HC), F32),
    }
    scratch = {
        "X": V((T, TB, D), BF), "Wq": V((DP, R, Cq), BF), "Wo": V((T, DP, R, C), BF),
        "Wu": V((T, NQ, 2, R, HC), BF), "Wd": V((T, NQ, 2, R, HC), BF), "BU": V((T, 1, HC), F32),
        "Q": V((RW, C), BF), "K": V((RW, C), BF), "V": V((RW, C), BF),
        "KT": V((C, RW), BF), "VT": V((C, RW), BF), "BIAS": V((RW, TB), F32),
        "CT": V((C, TB), F32), "LSE": V((T, hp, TB), F32), "CXR": V((T, TB, C), BF),
        "CTX": V((T, TB, C), BF), "FEED": V((2, TB, D), F32), "N1": V((TB, D), F32),
        "IV1": V((TB, 1), F32), "H1": V((TB, D), F32), "POOL": V((max(6, T), TB, D), BF),
        "MIDT": V((D, 2 * TB), BF), "PRE": V((TB, HC), F32), "ACT": V((T, 2 * TB, HC), BF),
        "SL": V((T, 2 * TB, HC), BF),
        "GFT": V((D, 2 * TB), BF),
        "GC": V((T, TB, C), BF),
        "DK": V((RW, C), F32), "DV": V((RW, C), F32), "DPJ": V((T, TB, Cq), BF),
        "g_ZB": V((T + 1, TB, D), BF), "RWO": V((T, NQ, R, C), BF), "RQ": V((NQ, R, Cq), BF),
        "FSW": V((2, R, HC), BF),
        "q_HB": V((1, 2, R // 2, Cq), BF), "q_FB": V((1, 2, S - 1, R, Cq), BF),
        "o_HB": V((T, 2, R // 2, C), BF), "o_FB": V((T, 2, S - 1, R, C), BF), "o_ZB": V((T + 1, R, C), BF),
        "u_HB": V((T, 2, R, HC), BF), "u_FB": V((T, 2, S - 1, 2, R, HC), BF), "u_ZB": V((T + 1, 2, R, HC), BF),
        "d_HB": V((T, 2, R, HC), BF), "d_FB": V((T, 2, S - 1, 2, R, HC), BF), "d_ZB": V((T + 1, 2, R, HC), BF),
        "SACC": V((6, 8, D), F32), "SBA": V((8, HC), F32),
        "SV": V((8, D), F32), "SV1": V((8, D), F32), "SV2": V((NQ, 8, D), F32), "SV3": V((T, 8, D), F32),
        "SB": V((2 * T, 1, HC), F32), "SB1": V((2 * T, 1, HC), F32), "SB2": V((NQ, 2 * T, 1, HC), F32),
        "SB3": V((T, 2 * T, 1, HC), F32),
        "SQ": V((8, C), F32), "SQ1": V((8, C), F32), "SQ2": V((NQ, 8, C), F32),
        "t_zs": dma((T, 2)), "t_zr": dma((T,)),
        "q_rs": dma((1, 2, S)), "q_rr": dma((1, 2, S)), "q_gs": dma((1, 2, S)), "q_gr": dma((1, 2, S)),
        "tw_s": dma((2,)), "tw_r": dma((2,)), "sw_s": dma((2,)), "sw_r": dma((2,)),
        "b_s": dma((T,)), "b_r": dma((T,)), "c_s": dma((T,)), "c_r": dma((T,)),
        "e_s": dma((4,)), "e_r": dma((4,)), "gc_s": dma((T,)), "gc_r": dma((T,)),
        "go_s": dma((2,)), "go_r": dma((2,)), "g_cs": dma((T,)), "g_cr": dma((T + 1,)),
        "a_s": dma((1, 3)), "a_r": dma((1, 3)),
        "ag_s": dma((2, 3, max(NQ, T))), "ag_r": dma((2, 3, max(NQ, T))),
        "fs_s": dma((2,)), "fs_r": dma((2,)), "in_s": dma((2,)),
    }
    for n in "oud":
        scratch[n + "_zs"] = dma((T, 2))
        scratch[n + "_zr"] = dma((T,))
        for m in ("_rs", "_rr", "_gs", "_gr"):
            scratch[n + m] = dma((T, 2, S))
        scratch[n + "_cs"] = dma((T,))
        scratch[n + "_cr"] = dma((T + 1,))
    names = ins + list(outs) + list(scratch)
    vm = pl.BlockSpec(memory_space=pltpu.VMEM)
    return pl.pallas_call(
        functools.partial(layer_kernel, cf, names),
        out_shape=tuple(jax.ShapeDtypeStruct(s, k) for s, k in outs.values()),
        in_specs=[pl.BlockSpec(memory_space=pl.ANY)] * 2 + [vm] * (len(ins) - 2),
        out_specs=(vm,) * len(outs),
        scratch_shapes=list(scratch.values()),
        compiler_params=pltpu.CompilerParams(
            collective_id=0, has_side_effects=True, vmem_limit_bytes=VMEM_LIMIT
        ),
        name="layer",
    )(*args)


def shards(
    tokens, segment_ids, out_grad, w_qkv, b_qv, w_out, b_out, norm1_gain, norm1_bias,
    w_up, b_up, w_down, b_down, norm2_gain, norm2_bias,
):
    DP, T = lax.axis_size("dp"), lax.axis_size("tensor")
    TB, D = tokens.shape
    R, _, C = w_qkv.shape
    HC = w_up.shape[1] // 2
    RW = segment_ids.shape[1]
    cf = SimpleNamespace(T=T, NQ=DP // 2, TB=TB, D=D, R=R, C=C, HC=HC, DP=DP)
    bq = b_qv.astype(F32)
    bqkv = jnp.concatenate([bq[0:1], jnp.zeros_like(bq[0:1]), bq[1:2]], axis=1)
    vecs = jnp.stack(
        [b_out, norm1_gain, norm1_bias, b_down, norm2_gain, norm2_bias, b_out, b_out]
    ).astype(F32)
    segc = jnp.broadcast_to(segment_ids[0][:, None], (RW, 128))
    segr = segment_ids.reshape(T, 1, TB)
    res = layer(
        cf, tokens, out_grad, w_qkv.reshape(R, 3 * C), w_out.T, w_up, w_down.T, bqkv,
        b_up.astype(F32).reshape(2, 1, HC), vecs, segc, segr,
    )
    out, gtok, gwq, gwo, gwu, gwd, sv, sbq, sbu = res
    return (
        out, gtok, gwq.reshape(R, 3, C), sbq[0:2], gwo.T, sv[5], sv[3], sv[4],
        gwu, sbu.reshape(2 * HC), gwd.T, sv[2], sv[0], sv[1],
    )


def solution(mesh):
    tok = P(("dp", "tensor"), None)
    in_specs = (
        tok, P("dp", None), tok, P("dp", None, "tensor"), P(None, "tensor"), P("tensor", "dp"),
        P(), P(), P(), P("dp", "tensor"), P("tensor"), P("tensor", "dp"), P(), P(), P(),
    )
    out_specs = (
        tok, tok, P("dp", None, "tensor"), P(None, "tensor"), P("tensor", "dp"),
        P(), P(), P(), P("dp", "tensor"), P("tensor"), P("tensor", "dp"), P(), P(), P(),
    )
    return jax.shard_map(shards, mesh=mesh, in_specs=in_specs, out_specs=out_specs, check_vma=False)
```

time: 709 us -> 292 us (0.41); the launches traced: 700 us -> 291 us
  waiting for transfers between devices: 440 us -> 0 us
  Pallas kernels: 0 us -> 267 us
  matrix products: 114 us -> 0 us
  blocking collectives: 54.2 us -> 0 us
  other arithmetic: 45.3 us -> 2.48 us
  between operations: 14.7 us -> 0.71 us
  local copies, waits for them, and re-layouts: 29.2 us -> 21.2 us
    pallas_call x0 -> x1, Pallas kernels: none -> 267 us  [layer(): pl.pallas_call(functools.partial(layer_kernel, cf, names), out_shape=tupl...]
    all_gather x7 -> x0, waiting for transfers between devices: 220 us -> none  [the longest x1 47.7 us: shards(): mid_rows = lax.all_gather(hidden_low, 'tensor', axis=0, tiled=True)]
    reduce_scatter x6 -> x0, waiting for transfers between devices: 218 us -> none  [the longest x1 44.1 us: shards(): lax.psum_scatter(transposed(grad_projected, flat_qkv).astype(jnp.bfloat16...]
    dot_general x26 -> x0, matrix products: 114 us -> none  [the longest x4 18.4 us: transposed(): lax.dot_general(left_side, right_side, (((1,), (1,)), ((), ())), preferre...]
    psum x1 -> x0, blocking collectives: 40.7 us -> none  [shards(): lax.psum((bias_qv_full, bias_up_full, grad_b_out, grad_gain_one, grad_bia...]
    reduce_sum x12 -> x0, other arithmetic: 23.2 us -> none  [the longest x2 7.09 us: one_block(): totals = jnp.sum(expd, axis=-1, keepdims=True)]
    convert_element_type x18 -> x1, other arithmetic: 17.7 us -> 0.62 us  [shards(): vecs = jnp.stack([b_out, norm1_gain, norm1_bias, b_down, norm2_gain, norm...]
    all_gather x1 -> x0, blocking collectives: 13.5 us -> none  [shards(): lax.all_gather(w_out, 'dp', axis=1, tiled=True)]
  transfers between devices with their start and end apart: 15 -> 0, of which waited for: 13 -> 0; matrix products, arithmetic and copies ran while one was open for 17% -> 0% of each run, Pallas kernels for 0% -> 0%
where the time goes in v1:
time: 292 us; the launch traced here: 291 us
  Pallas kernels  267 us (91%)
  local copies, waits for them, and re-layouts  21.2 us (7%)
    pallas_call x1, Pallas kernels, layer(): pl.pallas_call(functools.partial(layer_kernel, cf, names), out_shape=tupl...  267 us
    unnamed x26, local copies, waits for them, and re-layouts  10.3 us

profile of v1, /device:TPU:0, one launch (start us, length us, event | category | flops | bytes accessed | tf_op | source)
XLA Modules:
  0.0 291.3 jit_solution(5384390357702636092)
XLA Ops:
  0.7 0.8 fusion.2
  2.0 0.7 stack.23
  2.7 0.7 stack.24
  3.4 0.7 stack.25
  4.1 1.3 reshape.52
  5.3 0.7 stack.26
  6.0 0.7 stack.27
  6.7 0.7 stack.28
  7.5 0.6 convert_element_type.8.refs_8_
  8.1 1.6 copy.36
  9.8 0.8 copy.38.refs_2_
  10.8 0.8 copy.37
  11.6 1.0 broadcast_in_dim.12.refs_9_
  12.6 266.9 %layer.1 = (bf16[256,1024]{1,0:T(8,128)(2,1)}, bf16[256,1024]{1,0:T(8,128)(2,1)}, f32[128,768]{1,0:T(8,128)}, f32[128,256]{1,0:T(8,128)}, f32[128,1024]{1,0:T(8,...) custom-call(bf16[256,1024]{1,0:T(8,128)(2,1)} %refs_0_.1, ...), custom_call_target="tpu_custom_call" | custom-call | tf_op jit(solution)/shard_map/layer/pallas_call | solution.py:918
  279.5 1.3 slice.29
  280.8 1.7 fusion.1
  282.5 1.7 copy.41
  284.2 1.1 copy.39
  285.3 0.9 copy.40
  286.4 1.0 copy.42
  287.4 0.8 copy.47
  288.6 0.8 copy.48
  289.9 0.8 copy.49
  290.7 0.6 copy.50
  (21 shorter events, 2.0 us)
Async XLA Ops:
  0.6 9.0 %copy-start.5 = (bf16[128,3,256]{2,0,1:T(8,128)(2,1)S(1)}, bf16[128,3,256]{2,0,1:T(8,128)(2,1)}, u32[]{:S(2)}) copy-start(bf16[128,3,256]{2,0,1:T(8,128)(2,1)} %param.18) | copy-start | bytes 589828
  9.8 1.0 copy-start.4
  10.8 0.9 copy-start.6
  285.3 1.0 copy-start.3
  286.4 1.0 copy-start.2
  287.4 1.2 copy-start.1
  288.6 1.2 copy-start
  289.9 0.8 copy-start.7

commit v2 on v1

--- a/solution.py
+++ b/solution.py
@@ -234,16 +234,25 @@
         copy(k.ZB.at[slot], k.ZB.at[slot], k.cs.at[tt], k.cr.at[slot], partner).wait_recv()
         add(k.piece(tt, q), k.ZB.at[slot])
 
-    def chain(k, tt):
-        @pl.when(((tt >= t) & (t > 0)) | ((tt < t) & (t < T - 1)))
+    def chain_first(k, tt):
+        @pl.when(((tt > t) & (t == 0)) | ((tt < t) & (t == T - 1)))
+        def _():
+            chain_send(k, tt)
+
+    def chain_on(k, tt):
+        @pl.when(((tt > t) & (t > 0)) | ((tt < t) & (t < T - 1)))
         def _():
             chain_take(k, tt, tt)
-
-        @pl.when((tt == t) & (t < T - 1))
-        def _():
-            chain_take(k, tt, T)
-
-        chain_send(k, tt)
+            chain_send(k, tt)
+
+    def chain_end(k):
+        @pl.when(t > 0)
+        def _():
+            chain_take(k, t, t)
+
+        @pl.when(t < T - 1)
+        def _():
+            chain_take(k, t, T)
 
     barrier = pltpu.get_barrier_semaphore()
     peers = [partner]
@@ -251,33 +260,65 @@
     peers += [(d, lax.rem(t + k, T)) for k in range(1, T)]
     for peer in peers:
         pl.semaphore_signal(barrier, inc=1, device_id=peer, device_id_type=MESH)
-    get_tok = pltpu.make_async_copy(r.tok, r.X.at[t], r.in_s.at[0])
-    get_tok.start()
-    get_og = pltpu.make_async_copy(r.og, r.out, r.in_s.at[1])
-    get_og.start()
-    r.Wq[d] = r.wq[...]
-    r.Wo[t, d] = r.wo[...]
+    gets = [
+        pltpu.make_async_copy(r.tok, r.X.at[t], r.in_s.at[0]),
+        pltpu.make_async_copy(r.og, r.out, r.in_s.at[1]),
+    ]
+    for n in range(3):
+        gets.append(
+            pltpu.make_async_copy(r.wq.at[n], r.Wq.at[d, :, pl.ds(n * C, C)], r.in_s.at[2 + n])
+        )
+    for get in gets:
+        get.start()
     lo = pl.multiple_of(c * HC, 128)
+    ro = pl.multiple_of(oc * HC, 128)
+
+    def flipped(x):
+        return x.astype(F32).T.astype(BF)
+
+    r.Wo[t, d] = flipped(r.wo[...])
+    r.FSW[0] = r.wu[:, pl.ds(ro, HC)]
+    r.FSW[1] = flipped(r.wd[pl.ds(ro, HC), :])
     r.Wu[t, q, c] = r.wu[:, pl.ds(lo, HC)]
-    r.Wd[t, q, c] = r.wd[:, pl.ds(lo, HC)]
-    ro = pl.multiple_of(oc * HC, 128)
-    r.FSW[0] = r.wu[:, pl.ds(ro, HC)]
-    r.FSW[1] = r.wd[:, pl.ds(ro, HC)]
-    r.BU[t] = r.bup[c]
-    get_tok.wait()
-    get_og.wait()
+    r.Wd[t, q, c] = flipped(r.wd[pl.ds(lo, HC), :])
+    r.BU[t] = r.bup[...].astype(F32).reshape(1, 2 * HC)
+    for n, name in enumerate(("b_out", "g1", "n1", "b_down", "g2", "n2")):
+        r.vecs[n : n + 1, :] = getattr(r, name)[...].astype(F32).reshape(1, D)
+    r.segc[...] = jnp.broadcast_to(r.seg[...].astype(F32), (128, RW)).T
+    for get in gets:
+        get.wait()
     pl.semaphore_wait(barrier, len(peers))
 
-    z_send(kt, t)
+    swap_u = copy(r.FSW.at[0], r.Wu.at[t, q, c], r.sw_s.at[0], r.sw_r.at[0], partner)
+    swap_d = copy(r.FSW.at[1], r.Wd.at[t, q, c], r.sw_s.at[1], r.sw_r.at[1], partner)
+    swap_u.start()
     z_send(ko, t)
     twin_q(0, q)
     ring_send(kq, 0, 0)
-    swap_u = copy(r.FSW.at[0], r.Wu.at[t, q, c], r.sw_s.at[0], r.sw_r.at[0], partner)
-    swap_d = copy(r.FSW.at[1], r.Wd.at[t, q, c], r.sw_s.at[1], r.sw_r.at[1], partner)
-    swap_u.start()
     swap_d.start()
     twin_o(t, q)
     ring_send(ko, t, 0)
+
+    def swapped(n, ref):
+        ref = ref.at[t, q, oc]
+        copy(ref, ref, r.sw_s.at[n], r.sw_r.at[n], partner).wait_recv()
+
+    swapped(0, r.Wu)
+    z_send(ku, t)
+    z_send(kt, t)
+    ring_send(ku, t, 0)
+    swapped(1, r.Wd)
+
+    def weights_z(tt):
+        @pl.when(tt == 0)
+        def _():
+            z_right(kd_, t, "start")
+
+        @pl.when(tt == T - 1)
+        def _():
+            z_left(kd_, t, "start")
+
+    weights_z(t)
     for k in range(1, T):
         tt = lax.rem(t + k, T)
         copy(r.BU.at[t], r.BU.at[t], r.b_s.at[tt], r.b_r.at[t], (d, tt)).start()
@@ -285,25 +326,15 @@
     r.SB[...] = jnp.zeros_like(r.SB)
     r.DK[...] = jnp.zeros_like(r.DK)
     r.DV[...] = jnp.zeros_like(r.DV)
-    for n, (ref, w) in enumerate(((r.Wu, ku), (r.Wd, kd_))):
-        copy(ref.at[t, q, oc], ref.at[t, q, oc], r.sw_s.at[n], r.sw_r.at[n], partner).wait_recv()
-        ring_send(w, t, 0)
-
-    def weights_z(tt):
-        @pl.when(tt == 0)
-        def _():
-            z_right(ku, t, "start")
-
-        @pl.when(tt == T - 1)
-        def _():
-            z_left(ku, t, "start")
 
     def project(tt):
         x = r.X[tt]
         at = pl.ds(pl.multiple_of(tt * TB, TB), TB)
         for part, name in enumerate(("Q", "K", "V")):
             w = merge(r.Wq[:, :, part * C : (part + 1) * C])
-            y = nn(x, w) + r.bqkv[:, part * C : (part + 1) * C]
+            y = nn(x, w)
+            if part != 1:
+                y = y + r.bqv[part // 2 : part // 2 + 1, :].astype(F32)
             y = y.astype(BF)
             if part == 0:
                 r.Q[at, :] = y * jnp.asarray(HD ** (-0.5), BF)
@@ -314,58 +345,49 @@
                 r.V[at, :] = y
                 r.VT[:, at] = y.astype(F32).T.astype(BF)
 
-    weights_z(t)
-    for s in range(S):
-        arrived(kq, 0, s, twin_q)
-        if s + 1 < S:
-            ring_send(kq, 0, s + 1)
-    copy(r.RQ, r.RQ, r.tw_s.at[1], r.tw_r.at[1], partner).wait_recv()
-    project(t)
+    arrived(kq, 0, 0, twin_q)
+    ring_send(kq, 0, 1)
+    ring_send(kd_, t, 0)
     for j in range(1, T):
         tt = tp(j)
+        for k in (ko, ku):
+            z_wait(k, tt)
+            z_send(k, tt)
+            ring_send(k, tt, 0)
+        twin_o(tt, q)
+        ring_adv(ko, tp(j - 1), twin_o)
+        ring_adv(ku, tp(j - 1))
+        if j == 1:
+            for s in range(1, S):
+                arrived(kq, 0, s, twin_q)
+                if s + 1 < S:
+                    ring_send(kq, 0, s + 1)
+            copy(r.RQ, r.RQ, r.tw_s.at[1], r.tw_r.at[1], partner).wait_recv()
+            project(t)
+        else:
+            ring_fin(ko, tp(j - 2), twin_o)
         z_wait(kt, tt)
         z_send(kt, tt)
-        z_wait(ko, tt)
-        z_send(ko, tt)
         weights_z(tt)
-        twin_o(tt, q)
-        ring_send(ko, tt, 0)
-        ring_adv(ko, tp(j - 1), twin_o)
         if j == 1:
-            ring_adv(ku, t)
             ring_adv(kd_, t)
-        else:
-            ring_fin(ko, tp(j - 2), twin_o)
         project(tt)
     ring_adv(ko, tp(T - 1), twin_o)
-    if T > 1:
-        ring_fin(ko, tp(T - 2), twin_o)
+    ring_adv(ku, tp(T - 1))
+    ring_fin(ko, tp(T - 2), twin_o)
     ring_fin(ko, tp(T - 1), twin_o)
 
-    line = [(ku, j) for j in range(1, T)] + [(kd_, j) for j in range(1, T)]
-    done = [0]
-
-    def serve():
-        n = done[0]
-        done[0] += 1
-        if n > len(line):
-            return
-        if n > 0:
-            ring_adv(line[n - 1][0], tp(line[n - 1][1]))
-        if n < len(line):
-            k, j = line[n]
-            tt = tp(j)
-            z_wait(k, tt)
-            z_send(k, tt)
-            if n == 0:
-                z_send(kd_, t)
-            ring_send(k, tt, 0)
+    def take_down(j):
+        tt = tp(j)
+        z_wait(kd_, tt)
+        z_send(kd_, tt)
+        ring_send(kd_, tt, 0)
 
     lane = lax.broadcasted_iota(jnp.int32, (1, 128), 1)
     picks = [(lane < HD).astype(F32).astype(BF), (lane >= HD).astype(F32).astype(BF)]
 
     def bias_for(i):
-        same = r.segc[:, 0:1] == r.segr[i]
+        same = r.segc[:, 0:1] == r.seg[:, pl.ds(pl.multiple_of(i * TB, TB), TB)].astype(F32)
         r.BIAS[...] = jnp.where(same, 0.0, NEG)
 
     def attend(j):
@@ -389,9 +411,12 @@
             copy(r.CXR.at[i], r.CTX.at[t], r.c_s.at[i], r.c_r.at[t], (d, i)).start()
 
     spin(0, T // 2, attend)
-    serve()
+    take_down(1)
     spin(T // 2, T, attend)
-    serve()
+    for j in range(2, T):
+        take_down(j)
+        if j == 2:
+            ring_adv(kd_, tp(1))
     r.CTX[t] = r.CXR[t]
     for k in range(1, T):
         tt = lax.rem(t + k, T)
@@ -470,7 +495,7 @@
         tt = tp(j)
         ring_fin(ku, tt)
         w = merge(r.Wu[tt])
-        bias = r.BU[tt]
+        bias = r.BU[tt, :, pl.ds(lo, HC)]
 
         def block(b):
             r.PRE[...] = nn(r.POOL[MID + b], w) + bias
@@ -488,9 +513,10 @@
 
         spin(0, 2, block)
 
-    up(0)
-    for j in range(1, T):
-        serve()
+    for j in range(T):
+        ahead = 2 if j == 0 else j + 1 if j >= 2 else T
+        if ahead < T:
+            ring_adv(kd_, tp(ahead))
         up(j)
     turn(MID, r.MIDT)
 
@@ -509,10 +535,7 @@
         spin(0, 2, block)
 
     for j in range(T):
-        serve()
         down(j)
-    while done[0] <= len(line):
-        serve()
 
     def give(n):
         def step(at):
@@ -589,6 +612,9 @@
         spin(0, 2, block)
         r.SB[pl.ds(2 * tt + c, 1)] = r.SBA[...].sum(axis=0, keepdims=True)[None]
 
+    def slot_weights(k):
+        tt = tp(T - 1 - k)
+
         def weight(qq):
             at = pl.ds(pl.multiple_of(qq * 2 * R, 2 * R), 2 * R)
             y = nn(r.GFT[at, :], r.ACT[tt])
@@ -600,7 +626,31 @@
         rs_send(kd_, tt, 0)
         rs_send(ku, tt, 0)
 
-    spin(0, T, slot_back)
+    def slot_both(k):
+        slot_back(k)
+        slot_weights(k)
+
+    H = T // 2
+
+    def far(k):
+        return tp(T - 1 - k)
+
+    def pair_mid(k):
+        rs_mid(kd_, far(k))
+        rs_mid(ku, far(k))
+
+    def pair_last(k):
+        for w in (kd_, ku):
+            rs_last(w, far(k))
+            chain_first(w, far(k))
+
+    def pair_on(k):
+        chain_on(kd_, far(k))
+        chain_on(ku, far(k))
+
+    spin(0, H, slot_both)
+    spin(H, T, slot_back)
+    pair_mid(0)
     give(3)
 
     def first_back(at):
@@ -632,22 +682,9 @@
         tt = lax.rem(t + k, T)
         copy(r.CXR.at[tt], r.CTX.at[t], r.c_s.at[tt], r.c_r.at[t], (d, tt)).wait_send()
     spin(0, T, context_back)
-    drain_gather(ko)
-    copy(r.RWO, r.RWO, r.tw_s.at[0], r.tw_r.at[0], partner).wait_send()
-
-    r.GFT[:, 0:TB] = r.gtok[...].astype(F32).T.astype(BF)
-
-    def out_back(tt):
-        def weight(qq):
-            at = pl.ds(pl.multiple_of(qq * 2 * R, 2 * R), 2 * R)
-            y = nn(r.GFT[at, 0:TB], r.CTX[tt]).astype(BF)
-            r.Wo[tt, pl.ds(2 * qq, 2)] = y.reshape(2, R, C)
-            copy(r.Wo.at[tt, 2 * qq + oc], r.RWO.at[tt, qq], r.go_s.at[0], r.go_r.at[0], partner).start()
-
-        spin(0, NQ, weight)
-
-    spin(0, T, out_back)
-
+    for k in range(1, H):
+        pair_mid(k)
+    spin(H, T, slot_weights)
     for n in range(6):
         r.SV[n : n + 1, :] = r.SACC[n].sum(axis=0, keepdims=True)
     r.SV[6:8, :] = jnp.zeros((2, D), F32)
@@ -690,18 +727,6 @@
     sum_core(0, r.SV, r.SV1, "start")
     sum_core(1, r.SB, r.SB1, "start")
 
-    copy(r.RWO, r.RWO, r.go_s.at[0], r.go_r.at[0], partner).wait_recv()
-
-    def out_join(k):
-        tt = tp(T - 1 - k)
-
-        def step(qq):
-            add(r.Wo.at[tt, 2 * qq + c], r.RWO.at[tt, qq])
-
-        spin(0, NQ, step)
-        rs_send(ko, tt, 0)
-
-    spin(0, T, out_join)
     sum_core(0, r.SV, r.SV1, "end")
     sum_core(1, r.SB, r.SB1, "end")
     sum_group(0, 0, r.SV, r.SV2, q, NQ, chip_dev, "start")
@@ -729,24 +754,21 @@
             r.DK[:, pair] += nn(ds, qh)
             r.CT[h * HD : (h + 1) * HD, :] = nn(r.KT[h * HD : (h + 1) * HD, :], ds) * HD ** (-0.5)
         r.DPJ[i, :, 0:C] = r.CT[...].T.astype(BF)
-        tt = tp(T - 1 - j)
-        rs_mid(kd_, tt)
-        rs_mid(ku, tt)
-        rs_mid(ko, tt)
-
-    spin(0, T, attend_back)
+
+    spin(0, H, attend_back)
+    pair_last(0)
+    spin(H, T, attend_back)
     sum_group(0, 0, r.SV, r.SV2, q, NQ, chip_dev, "end")
     sum_group(0, 1, r.SB, r.SB2, q, NQ, chip_dev, "end")
     sum_group(1, 0, r.SV, r.SV3, t, T, row_dev, "start")
     sum_group(1, 1, r.SB, r.SB3, t, T, row_dev, "start")
-
     exchange(0, MID, "drain")
     exchange(2, GF, "drain")
 
     r.SQ[...] = jnp.zeros_like(r.SQ)
 
     def input_back(k):
-        tt = tp(T - 1 - k)
+        tt = far(k)
         at = pl.ds(pl.multiple_of(tt * TB, TB), TB)
         r.DPJ[tt, :, C : 2 * C] = r.DK[at, :].astype(BF)
         r.DPJ[tt, :, 2 * C : 3 * C] = r.DV[at, :].astype(BF)
@@ -754,27 +776,53 @@
         r.SQ[1:2, :] += r.DPJ[tt, :, 2 * C : 3 * C].astype(F32).sum(axis=0, keepdims=True)
         r.POOL[tt] = nt(r.DPJ[tt], merge(r.Wq[...])).astype(BF)
 
-        @pl.when(tt != t)
-        def _():
-            chain(kg, tt)
+        @pl.when(k == 0)
+        def _():
+            chain_first(kg, tt)
 
     spin(0, T, input_back)
-
-    def settle(k, tt):
-        rs_last(k, tt)
-
-        @pl.when(tt != t)
-        def _():
-            chain(k, tt)
-
     sum_core(2, r.SQ, r.SQ1, "start")
-    settle(kd_, tp(T - 1))
-    settle(ku, tp(T - 1))
+    for k in range(1, H):
+        pair_last(k)
+    for k in range(1, T - 1):
+        chain_first(kg, far(k))
+    pair_on(0)
+    for k in range(H, T - 1):
+        pair_mid(k)
+    drain_gather(ko)
+    copy(r.RWO, r.RWO, r.tw_s.at[0], r.tw_r.at[0], partner).wait_send()
+
+    r.GFT[:, 0:TB] = r.gtok[...].astype(F32).T.astype(BF)
+
+    def out_back(tt):
+        def weight(qq):
+            at = pl.ds(pl.multiple_of(qq * 2 * R, 2 * R), 2 * R)
+            y = nn(r.GFT[at, 0:TB], r.CTX[tt]).astype(BF)
+            r.Wo[tt, pl.ds(2 * qq, 2)] = y.reshape(2, R, C)
+            copy(r.Wo.at[tt, 2 * qq + oc], r.RWO.at[tt, qq], r.go_s.at[0], r.go_r.at[0], partner).start()
+
+        spin(0, NQ, weight)
+
+    spin(0, T, out_back)
+
+    pair_mid(T - 1)
+    chain_on(kg, far(0))
+    copy(r.RWO, r.RWO, r.go_s.at[0], r.go_r.at[0], partner).wait_recv()
+
+    def out_join(k):
+        tt = tp(T - 1 - k)
+
+        def step(qq):
+            add(r.Wo.at[tt, 2 * qq + c], r.RWO.at[tt, qq])
+
+        spin(0, NQ, step)
+        rs_send(ko, tt, 0)
+
+    spin(0, T, out_join)
 
     copy(r.RQ, r.RQ, r.tw_s.at[1], r.tw_r.at[1], partner).wait_send()
     for s in range(S):
         ring_send(kq, 0, s, "drain")
-
     many = max(2, 256 // R)
 
     def qkv_weight(g):
@@ -798,13 +846,27 @@
 
     spin(0, NQ, q_join)
     rs_send(kq, 0, 0)
-    settle(ko, tp(T - 1))
-    for j in range(T - 2, 0, -1):
-        settle(kd_, tp(j))
-        settle(ku, tp(j))
-        settle(ko, tp(j))
-        if j == T - 2:
+    order = [2, 1] if T == 4 else list(range(1, T - 1))
+    for k in range(H, T - 1):
+        pair_last(k)
+    for n, k in enumerate(order):
+        pair_on(k)
+        if n > 0 or T != 4:
+            chain_on(kg, far(k))
+        else:
+            chain_on(kg, far(k))
+            for m in range(T):
+                rs_mid(ko, far(m))
             rs_mid(kq, 0)
+    if T != 4:
+        for m in range(T):
+            rs_mid(ko, far(m))
+        rs_mid(kq, 0)
+    for k in range(T - 1):
+        rs_last(ko, far(k))
+        chain_first(ko, far(k))
+    for k in range(T - 1):
+        chain_on(ko, far(k))
     rs_last(kd_, t)
     rs_last(ku, t)
     rs_last(ko, t)
@@ -812,29 +874,30 @@
     sum_group(1, 0, r.SV, r.SV3, t, T, row_dev, "end")
     sum_group(1, 1, r.SB, r.SB3, t, T, row_dev, "end")
     sum_group(0, 2, r.SQ, r.SQ2, q, NQ, chip_dev, "end")
-    chain(kg, t)
+    chain_end(kg)
 
     def finish(at):
         r.gtok[at, :] = (r.H1[at, :] + r.POOL[t, at, :].astype(F32)).astype(BF)
 
     rows_of(finish)
-    chain(kd_, t)
-    chain(ku, t)
-    chain(ko, t)
+    chain_end(kd_)
+    chain_end(ku)
+    chain_end(ko)
     cps = []
     for n, ref in enumerate((r.Wu, r.Wd)):
         cp = copy(ref.at[t, q, oc], r.FSW.at[n], r.fs_s.at[n], r.fs_r.at[n], partner)
         cp.start()
         cps.append(cp)
-    r.gwq[...] = r.Wq[d].astype(F32)
-    r.gwo[...] = r.Wo[t, d].astype(F32)
+    for n in range(3):
+        r.gwq[n] = r.Wq[d, :, n * C : (n + 1) * C]
+    r.gwo[...] = r.Wo[t, d]
     r.sv[...] = r.SV[...]
     r.sbq[...] = r.SQ[...]
     r.sbu[...] = r.SB[pl.ds(2 * t, 2)]
     for n, (ref, o) in enumerate(((r.Wu, r.gwu), (r.Wd, r.gwd))):
         copy(r.FSW.at[n], r.FSW.at[n], r.fs_s.at[n], r.fs_r.at[n], partner).wait_recv()
-        o[:, pl.ds(lo, HC)] = ref[t, q, c].astype(F32)
-        o[:, pl.ds(ro, HC)] = r.FSW[n].astype(F32)
+        o[:, pl.ds(lo, HC)] = ref[t, q, c]
+        o[:, pl.ds(ro, HC)] = r.FSW[n]
         cps[n].wait_send()
 
     def drain(tt):
@@ -866,15 +929,15 @@
     hp = -(-heads // 8) * 8
     dma = pltpu.SemaphoreType.DMA
     V = pltpu.VMEM
-    ins = ["tok", "og", "wq", "wo", "wu", "wd", "bqkv", "bup", "vecs", "segc", "segr"]
+    ins = ["tok", "og", "wq", "wo", "wu", "wd", "bqv", "bup", "b_out", "g1", "n1", "b_down", "g2", "n2", "seg"]
     outs = {
-        "out": ((TB, D), BF), "gtok": ((TB, D), BF), "gwq": ((R, Cq), F32), "gwo": ((R, C), F32),
-        "gwu": ((R, 2 * HC), F32), "gwd": ((R, 2 * HC), F32), "sv": ((8, D), F32),
+        "out": ((TB, D), BF), "gtok": ((TB, D), BF), "gwq": ((3, R, C), BF), "gwo": ((R, C), BF),
+        "gwu": ((R, 2 * HC), BF), "gwd": ((R, 2 * HC), BF), "sv": ((8, D), F32),
         "sbq": ((8, C), F32), "sbu": ((2, 1, HC), F32),
     }
     scratch = {
         "X": V((T, TB, D), BF), "Wq": V((DP, R, Cq), BF), "Wo": V((T, DP, R, C), BF),
-        "Wu": V((T, NQ, 2, R, HC), BF), "Wd": V((T, NQ, 2, R, HC), BF), "BU": V((T, 1, HC), F32),
+        "Wu": V((T, NQ, 2, R, HC), BF), "Wd": V((T, NQ, 2, R, HC), BF), "BU": V((T, 1, 2 * HC), F32), "vecs": V((8, D), F32), "segc": V((RW, 128), F32),
         "Q": V((RW, C), BF), "K": V((RW, C), BF), "V": V((RW, C), BF),
         "KT": V((C, RW), BF), "VT": V((C, RW), BF), "BIAS": V((RW, TB), F32),
         "CT": V((C, TB), F32), "LSE": V((T, hp, TB), F32), "CXR": V((T, TB, C), BF),
@@ -904,7 +967,7 @@
         "go_s": dma((2,)), "go_r": dma((2,)), "g_cs": dma((T,)), "g_cr": dma((T + 1,)),
         "a_s": dma((1, 3)), "a_r": dma((1, 3)),
         "ag_s": dma((2, 3, max(NQ, T))), "ag_r": dma((2, 3, max(NQ, T))),
-        "fs_s": dma((2,)), "fs_r": dma((2,)), "in_s": dma((2,)),
+        "fs_s": dma((2,)), "fs_r": dma((2,)), "in_s": dma((5,)),
     }
     for n in "oud":
         scratch[n + "_zs"] = dma((T, 2))
@@ -918,13 +981,46 @@
     return pl.pallas_call(
         functools.partial(layer_kernel, cf, names),
         out_shape=tuple(jax.ShapeDtypeStruct(s, k) for s, k in outs.values()),
-        in_specs=[pl.BlockSpec(memory_space=pl.ANY)] * 2 + [vm] * (len(ins) - 2),
+        in_specs=[pl.BlockSpec(memory_space=pl.ANY)] * 3 + [vm] * (len(ins) - 3),
         out_specs=(vm,) * len(outs),
         scratch_shapes=list(scratch.values()),
         compiler_params=pltpu.CompilerParams(
             collective_id=0, has_side_effects=True, vmem_limit_bytes=VMEM_LIMIT
         ),
         name="layer",
+    )(*args)
+
+
+def tail_kernel(cf, *refs):
+    src, dst = refs[:9], refs[9:]
+    out, gtok, gwq, gwo, gwu, gwd, sv, sbq, sbu = src
+    dst[0][...] = out[...]
+    dst[1][...] = gtok[...]
+    dst[2][...] = gwq[...].astype(F32)
+    dst[3][...] = sbq[0:2, :]
+    dst[4][...] = gwo[...].astype(F32).T
+    for n, row in ((5, 5), (6, 3), (7, 4), (11, 2), (12, 0), (13, 1)):
+        dst[n][...] = sv[row : row + 1, :].reshape(cf.D)
+    dst[8][...] = gwu[...].astype(F32)
+    for n in range(2):
+        dst[9][pl.ds(n * cf.HC, cf.HC)] = sbu[n].reshape(cf.HC)
+    dst[10][...] = gwd[...].astype(F32).T
+
+
+def tail(cf, *args):
+    R, C, D, HC, TB = cf.R, cf.C, cf.D, cf.HC, cf.TB
+    vm = pl.BlockSpec(memory_space=pltpu.VMEM)
+    shapes = [
+        ((TB, D), BF), ((TB, D), BF), ((3, R, C), F32), ((2, C), F32), ((C, R), F32),
+        ((D,), F32), ((D,), F32), ((D,), F32), ((R, 2 * HC), F32), ((2 * HC,), F32),
+        ((2 * HC, R), F32), ((D,), F32), ((D,), F32), ((D,), F32),
+    ]
+    return pl.pallas_call(
+        functools.partial(tail_kernel, cf),
+        out_shape=tuple(jax.ShapeDtypeStruct(*s) for s in shapes),
+        in_specs=[vm] * len(args),
+        out_specs=(vm,) * len(shapes),
+        name="tail",
     )(*args)
 
 
@@ -936,24 +1032,14 @@
     TB, D = tokens.shape
     R, _, C = w_qkv.shape
     HC = w_up.shape[1] // 2
-    RW = segment_ids.shape[1]
     cf = SimpleNamespace(T=T, NQ=DP // 2, TB=TB, D=D, R=R, C=C, HC=HC, DP=DP)
-    bq = b_qv.astype(F32)
-    bqkv = jnp.concatenate([bq[0:1], jnp.zeros_like(bq[0:1]), bq[1:2]], axis=1)
-    vecs = jnp.stack(
-        [b_out, norm1_gain, norm1_bias, b_down, norm2_gain, norm2_bias, b_out, b_out]
-    ).astype(F32)
-    segc = jnp.broadcast_to(segment_ids[0][:, None], (RW, 128))
-    segr = segment_ids.reshape(T, 1, TB)
     res = layer(
-        cf, tokens, out_grad, w_qkv.reshape(R, 3 * C), w_out.T, w_up, w_down.T, bqkv,
-        b_up.astype(F32).reshape(2, 1, HC), vecs, segc, segr,
+        cf, tokens, out_grad, w_qkv.transpose(1, 0, 2), w_out, w_up, w_down, b_qv, b_up,
+        b_out, norm1_gain, norm1_bias, b_down, norm2_gain, norm2_bias, segment_ids,
     )
-    out, gtok, gwq, gwo, gwu, gwd, sv, sbq, sbu = res
-    return (
-        out, gtok, gwq.reshape(R, 3, C), sbq[0:2], gwo.T, sv[5], sv[3], sv[4],
-        gwu, sbu.reshape(2 * HC), gwd.T, sv[2], sv[0], sv[1],
-    )
+    res = list(tail(cf, *res))
+    res[2] = res[2].transpose(1, 0, 2)
+    return tuple(res)
 
 
 def solution(mesh):

time: 292 us -> 248 us (0.85)
  local copies, waits for them, and re-layouts: 21.2 us -> 0 us
  Pallas kernels: 267 us -> 247 us
    pallas_call x1, Pallas kernels: 267 us -> 244 us  [layer(): pl.pallas_call(functools.partial(layer_kernel, cf, names), out_shape=tupl...]
    unnamed x26 -> x0, local copies, waits for them, and re-layouts: 10.3 us -> none
    another operation x7 -> x0, local copies, waits for them, and re-layouts: 4.17 us -> none  [shards(): jnp.stack([b_out, norm1_gain, norm1_bias, b_down, norm2_gain, norm2_bias,...]
    slice x3 -> x0, local copies, waits for them, and re-layouts: 3.73 us -> none  [the longest x1 1.69 us: shards(): sv[1]]
    pallas_call x0 -> x1, Pallas kernels: none -> 3.11 us  [tail(): pl.pallas_call(functools.partial(tail_kernel, cf), out_shape=tuple((jax.S...]
where the time goes in v2:
time: 248 us
  Pallas kernels  247 us (100%)
    pallas_call x1, Pallas kernels, layer(): pl.pallas_call(functools.partial(layer_kernel, cf, names), out_shape=tupl...  244 us

profile of v2, /device:TPU:0, one launch (start us, length us, event | category | flops | bytes accessed | tf_op | source)
XLA Modules:
  0.0 248.2 jit_solution(10480188097778945602)
XLA Ops:
  0.7 244.2 %layer.1 = (bf16[256,1024]{1,0:T(8,128)(2,1)}, bf16[256,1024]{1,0:T(8,128)(2,1)}, bf16[3,128,256]{2,1,0:T(8,128)(2,1)}, bf16[128,256]{1,0:T(8,128)(2,1)}, bf16[1...) custom-call(bf16[256,1024]{1,0:T(8,128)(2,1)} %refs_0_.1, ...), custom_call_target="tpu_custom_call" | custom-call | tf_op jit(solution)/shard_map/layer/pallas_call | solution.py:981
  244.9 3.1 %tail.1 = (bf16[256,1024]{1,0:T(8,128)(2,1)}, bf16[256,1024]{1,0:T(8,128)(2,1)}, f32[3,128,256]{2,1,0:T(8,128)}, f32[2,256]{1,0:T(2,128)}, f32[256,128]{1,0:T(8,...) custom-call(bf16[256,1024]{1,0:T(8,128)(2,1)} %get-tuple-element.37., ...), custom_call_target="tpu_custom_call" | custom-call | tf_op jit(solution)/shard_map/tail/pallas_call | solution.py:1018

commit v3 on v2

--- a/solution.py
+++ b/solution.py
@@ -10,6 +10,7 @@
 from jax.sharding import PartitionSpec as P
 
 HD = 64
+SEG_MOST = 512
 MESH = pl.DeviceIdType.MESH
 BF = jnp.bfloat16
 F32 = jnp.float32
@@ -326,6 +327,9 @@
     r.SB[...] = jnp.zeros_like(r.SB)
     r.DK[...] = jnp.zeros_like(r.DK)
     r.DV[...] = jnp.zeros_like(r.DV)
+    r.AM[...] = jnp.full_like(r.AM, NEG)
+    r.AL[...] = jnp.zeros_like(r.AL)
+    r.ACC[...] = jnp.zeros_like(r.ACC)
 
     def project(tt):
         x = r.X[tt]
@@ -345,16 +349,91 @@
                 r.V[at, :] = y
                 r.VT[:, at] = y.astype(F32).T.astype(BF)
 
+    lane = lax.broadcasted_iota(jnp.int32, (1, 128), 1)
+    picks = [(lane < HD).astype(F32).astype(BF), (lane >= HD).astype(F32).astype(BF)]
+    reach = (SEG_MOST - 2) // TB + 1
+
+    def rows_at(i):
+        return pl.ds(pl.multiple_of(i * TB, TB), TB)
+
+    def seg_row(i):
+        return r.seg[:, rows_at(i)].astype(F32)
+
+    def pair_up(i, b):
+        bias = jnp.where(r.segc[rows_at(b), 0:1] == seg_row(i), 0.0, NEG)
+        pairs = [slice((h // 2) * 128, (h // 2) * 128 + 128) for h in range(heads)]
+        owns = [slice(h * HD, (h + 1) * HD) for h in range(heads)]
+        before = [r.AM[i, h : h + 1, :] for h in range(heads)]
+        sums = [r.AL[i, h : h + 1, :] for h in range(heads)]
+        scs = [
+            nt(r.K[rows_at(b), pairs[h]], r.Q[rows_at(i), pairs[h]] * picks[h % 2]) + bias
+            for h in range(heads)
+        ]
+        tops = [jnp.maximum(before[h], jnp.max(scs[h], axis=0, keepdims=True)) for h in range(heads)]
+        es = [jnp.exp(scs[h] - tops[h]) for h in range(heads)]
+        shrinks = [jnp.exp(before[h] - tops[h]) for h in range(heads)]
+        news = [nn(r.VT[owns[h], rows_at(b)], es[h].astype(BF)) for h in range(heads)]
+        for h in range(heads):
+            r.AM[i, h : h + 1, :] = tops[h]
+            r.AL[i, h : h + 1, :] = sums[h] * shrinks[h] + jnp.sum(es[h], axis=0, keepdims=True)
+            r.ACC[i, owns[h], :] = r.ACC[i, owns[h], :] * shrinks[h] + news[h]
+
+    def attend(j):
+        new = tp(j)
+
+        def one(n):
+            other = tp(lax.div(n, 2))
+            side = lax.rem(n, 2)
+            i = other + (new - other) * side
+            b = new + (other - new) * side
+
+            @pl.when((i - b <= reach) & (b - i <= reach))
+            def _():
+                pair_up(i, b)
+
+        spin(0, 2 * j + 1, one)
+
+    def finish_context(j):
+        i = lax.rem(t + 1 + j, T)
+        for h in range(heads):
+            own = slice(h * HD, (h + 1) * HD)
+            r.CT[own, :] = r.ACC[i, own, :] / r.AL[i, h : h + 1, :]
+        r.AM[i, 0:heads, :] = r.AM[i, 0:heads, :] + jnp.log(r.AL[i, 0:heads, :])
+        r.CXR[i] = r.CT[...].T.astype(BF)
+
+        @pl.when(i != t)
+        def _():
+            copy(r.CXR.at[i], r.CTX.at[t], r.c_s.at[i], r.c_r.at[t], (d, i)).start()
+
+    def bias_for(i):
+        r.BIAS[...] = jnp.where(r.segc[:, 0:1] == seg_row(i), 0.0, NEG)
+
     arrived(kq, 0, 0, twin_q)
     ring_send(kq, 0, 1)
     ring_send(kd_, t, 0)
-    for j in range(1, T):
-        tt = tp(j)
+    def at_distance(k, take):
+        @pl.when(t - k >= 0)
+        def _():
+            take(t - k)
+
+        @pl.when(t + k < T)
+        def _():
+            take(t + k)
+
+    def take_weights(tt):
         for k in (ko, ku):
             z_wait(k, tt)
             z_send(k, tt)
             ring_send(k, tt, 0)
         twin_o(tt, q)
+
+    def take_tokens(tt):
+        z_wait(kt, tt)
+        z_send(kt, tt)
+        weights_z(tt)
+
+    for j in range(1, T):
+        at_distance(j, take_weights)
         ring_adv(ko, tp(j - 1), twin_o)
         ring_adv(ku, tp(j - 1))
         if j == 1:
@@ -364,18 +443,16 @@
                     ring_send(kq, 0, s + 1)
             copy(r.RQ, r.RQ, r.tw_s.at[1], r.tw_r.at[1], partner).wait_recv()
             project(t)
+            attend(0)
         else:
             ring_fin(ko, tp(j - 2), twin_o)
-        z_wait(kt, tt)
-        z_send(kt, tt)
-        weights_z(tt)
+        at_distance(j, take_tokens)
         if j == 1:
             ring_adv(kd_, t)
-        project(tt)
-    ring_adv(ko, tp(T - 1), twin_o)
-    ring_adv(ku, tp(T - 1))
-    ring_fin(ko, tp(T - 2), twin_o)
-    ring_fin(ko, tp(T - 1), twin_o)
+        project(tp(j))
+        attend(j)
+    inner = (t > 0) & (t < T - 1)
+    edge = (t == 0) | (t == T - 1)
 
     def take_down(j):
         tt = tp(j)
@@ -383,40 +460,20 @@
         z_send(kd_, tt)
         ring_send(kd_, tt, 0)
 
-    lane = lax.broadcasted_iota(jnp.int32, (1, 128), 1)
-    picks = [(lane < HD).astype(F32).astype(BF), (lane >= HD).astype(F32).astype(BF)]
-
-    def bias_for(i):
-        same = r.segc[:, 0:1] == r.seg[:, pl.ds(pl.multiple_of(i * TB, TB), TB)].astype(F32)
-        r.BIAS[...] = jnp.where(same, 0.0, NEG)
-
-    def attend(j):
-        i = lax.rem(t + 1 + j, T)
-        at = pl.ds(pl.multiple_of(i * TB, TB), TB)
-        bias_for(i)
-        for h in range(heads):
-            pair = slice((h // 2) * 128, (h // 2) * 128 + 128)
-            qh = r.Q[at, pair] * picks[h % 2]
-            sc = nt(r.K[:, pair], qh) + r.BIAS[...]
-            top = jnp.max(sc, axis=0, keepdims=True)
-            e = jnp.exp(sc - top)
-            total = jnp.sum(e, axis=0, keepdims=True)
-            ct = nn(r.VT[h * HD : (h + 1) * HD, :], e.astype(BF))
-            r.CT[h * HD : (h + 1) * HD, :] = ct / total
-            r.LSE[i, h : h + 1, :] = top + jnp.log(total)
-        r.CXR[i] = r.CT[...].T.astype(BF)
-
-        @pl.when(i != t)
-        def _():
-            copy(r.CXR.at[i], r.CTX.at[t], r.c_s.at[i], r.c_r.at[t], (d, i)).start()
-
-    spin(0, T // 2, attend)
+    spin(0, T, finish_context)
+    ring_adv(ko, tp(T - 1), twin_o)
+    ring_adv(ku, tp(T - 1))
+    ring_fin(ko, tp(T - 2), twin_o)
+    ring_fin(ko, tp(T - 1), twin_o)
     take_down(1)
-    spin(T // 2, T, attend)
-    for j in range(2, T):
-        take_down(j)
-        if j == 2:
-            ring_adv(kd_, tp(1))
+
+    @pl.when(inner)
+    def _():
+        for j in range(2, T):
+            take_down(j)
+            if j == 2:
+                ring_adv(kd_, tp(1))
+
     r.CTX[t] = r.CXR[t]
     for k in range(1, T):
         tt = lax.rem(t + k, T)
@@ -479,6 +536,14 @@
         copy(ref, ref, r.e_s.at[n], r.e_r.at[n], partner).wait_recv()
 
     exchange(0, MID)
+
+    @pl.when(edge)
+    def _():
+        for j in range(2, T):
+            take_down(j)
+            if j == 2:
+                ring_adv(kd_, tp(1))
+
     for k in range(1, T):
         tt = lax.rem(t + k, T)
         copy(r.BU.at[tt], r.BU.at[tt], r.b_s.at[tt], r.b_r.at[tt], partner).wait_recv()
@@ -615,20 +680,25 @@
     def slot_weights(k):
         tt = tp(T - 1 - k)
 
-        def weight(qq):
+        def down_weight(qq):
             at = pl.ds(pl.multiple_of(qq * 2 * R, 2 * R), 2 * R)
-            y = nn(r.GFT[at, :], r.ACT[tt])
-            r.Wd[tt, qq] = y.astype(BF).reshape(2, R, HC)
-            y = nn(r.MIDT[at, :], r.SL[tt])
-            r.Wu[tt, qq] = y.astype(BF).reshape(2, R, HC)
-
-        spin(0, NQ, weight)
-        rs_send(kd_, tt, 0)
-        rs_send(ku, tt, 0)
-
-    def slot_both(k):
-        slot_back(k)
-        slot_weights(k)
+            r.Wd[tt, qq] = nn(r.GFT[at, :], r.ACT[tt]).astype(BF).reshape(2, R, HC)
+
+        def up_weight(qq):
+            at = pl.ds(pl.multiple_of(qq * 2 * R, 2 * R), 2 * R)
+            r.Wu[tt, qq] = nn(r.MIDT[at, :], r.SL[tt]).astype(BF).reshape(2, R, HC)
+
+        spin(0, NQ, down_weight)
+
+        @pl.when(k < T - 1)
+        def _():
+            rs_send(kd_, tt, 0)
+
+        spin(0, NQ, up_weight)
+
+        @pl.when(k < T - 1)
+        def _():
+            rs_send(ku, tt, 0)
 
     H = T // 2
 
@@ -648,9 +718,26 @@
         chain_on(kd_, far(k))
         chain_on(ku, far(k))
 
-    spin(0, H, slot_both)
-    spin(H, T, slot_back)
-    pair_mid(0)
+    def part_last(w, k):
+        rs_last(w, far(k))
+        chain_first(w, far(k))
+
+    def slots(k):
+        slot_back(k)
+
+        @pl.when(k == 0)
+        def _():
+            slot_weights(k)
+
+        @pl.when(k == 1)
+        def _():
+            rs_mid(kd_, far(0))
+
+        @pl.when(k == 2)
+        def _():
+            rs_mid(ku, far(0))
+
+    spin(0, T, slots)
     give(3)
 
     def first_back(at):
@@ -682,9 +769,8 @@
         tt = lax.rem(t + k, T)
         copy(r.CXR.at[tt], r.CTX.at[t], r.c_s.at[tt], r.c_r.at[t], (d, tt)).wait_send()
     spin(0, T, context_back)
-    for k in range(1, H):
-        pair_mid(k)
-    spin(H, T, slot_weights)
+    spin(1, H, slot_weights)
+    part_last(kd_, 0)
     for n in range(6):
         r.SV[n : n + 1, :] = r.SACC[n].sum(axis=0, keepdims=True)
     r.SV[6:8, :] = jnp.zeros((2, D), F32)
@@ -727,13 +813,10 @@
     sum_core(0, r.SV, r.SV1, "start")
     sum_core(1, r.SB, r.SB1, "start")
 
-    sum_core(0, r.SV, r.SV1, "end")
-    sum_core(1, r.SB, r.SB1, "end")
-    sum_group(0, 0, r.SV, r.SV2, q, NQ, chip_dev, "start")
-    sum_group(0, 1, r.SB, r.SB2, q, NQ, chip_dev, "start")
+    outer = ind(t, 0, T) + ind(t, T - 1, T)
 
     def attend_back(j):
-        i = tp(j)
+        i = tp(j) + (tp(T - 1 - j) - tp(j)) * outer
         at = pl.ds(pl.multiple_of(i * TB, TB), TB)
 
         @pl.when(i != t)
@@ -745,7 +828,7 @@
             pair = slice((h // 2) * 128, (h // 2) * 128 + 128)
             qh = r.Q[at, pair] * picks[h % 2]
             gh = r.GC[i, :, pair] * picks[h % 2]
-            pr = jnp.exp(nt(r.K[:, pair], qh) + r.BIAS[...] - r.LSE[i, h : h + 1, :])
+            pr = jnp.exp(nt(r.K[:, pair], qh) + r.BIAS[...] - r.AM[i, h : h + 1, :])
             gp = nt(r.V[:, pair], gh)
             r.DV[:, pair] += nn(pr.astype(BF), gh)
             prod = pr * gp
@@ -755,13 +838,6 @@
             r.CT[h * HD : (h + 1) * HD, :] = nn(r.KT[h * HD : (h + 1) * HD, :], ds) * HD ** (-0.5)
         r.DPJ[i, :, 0:C] = r.CT[...].T.astype(BF)
 
-    spin(0, H, attend_back)
-    pair_last(0)
-    spin(H, T, attend_back)
-    sum_group(0, 0, r.SV, r.SV2, q, NQ, chip_dev, "end")
-    sum_group(0, 1, r.SB, r.SB2, q, NQ, chip_dev, "end")
-    sum_group(1, 0, r.SV, r.SV3, t, T, row_dev, "start")
-    sum_group(1, 1, r.SB, r.SB3, t, T, row_dev, "start")
     exchange(0, MID, "drain")
     exchange(2, GF, "drain")
 
@@ -776,19 +852,39 @@
         r.SQ[1:2, :] += r.DPJ[tt, :, 2 * C : 3 * C].astype(F32).sum(axis=0, keepdims=True)
         r.POOL[tt] = nt(r.DPJ[tt], merge(r.Wq[...])).astype(BF)
 
-        @pl.when(k == 0)
+        @pl.when(jnp.int32(k) < 2)
         def _():
             chain_first(kg, tt)
 
-    spin(0, T, input_back)
-    sum_core(2, r.SQ, r.SQ1, "start")
+    spin(0, H, attend_back)
+    part_last(ku, 0)
     for k in range(1, H):
-        pair_last(k)
-    for k in range(1, T - 1):
-        chain_first(kg, far(k))
-    pair_on(0)
+        pair_mid(k)
+    spin(H, T - 1, slot_weights)
+    sum_core(0, r.SV, r.SV1, "end")
+    sum_core(1, r.SB, r.SB1, "end")
+    sum_group(0, 0, r.SV, r.SV2, q, NQ, chip_dev, "start")
+    sum_group(0, 1, r.SB, r.SB2, q, NQ, chip_dev, "start")
+
+    def attend_late(j):
+        attend_back(j)
+        if T - 1 > reach:
+
+            @pl.when((j == T - 2) & edge)
+            def _():
+                input_back(0)
+
+    spin(H, T, attend_late)
+    def input_rest(k):
+        @pl.when((k > 0) | inner | (T - 1 <= reach))
+        def _():
+            input_back(k)
+
+    spin(0, T, input_rest)
+    spin(T - 1, T, slot_weights)
     for k in range(H, T - 1):
         pair_mid(k)
+    sum_core(2, r.SQ, r.SQ1, "start")
     drain_gather(ko)
     copy(r.RWO, r.RWO, r.tw_s.at[0], r.tw_r.at[0], partner).wait_send()
 
@@ -805,8 +901,7 @@
 
     spin(0, T, out_back)
 
-    pair_mid(T - 1)
-    chain_on(kg, far(0))
+    pair_on(0)
     copy(r.RWO, r.RWO, r.go_s.at[0], r.go_r.at[0], partner).wait_recv()
 
     def out_join(k):
@@ -846,25 +941,35 @@
 
     spin(0, NQ, q_join)
     rs_send(kq, 0, 0)
+    rs_send(kd_, t, 0)
+    rs_send(ku, t, 0)
+    chain_on(kg, far(0))
+    for k in range(1, H):
+        pair_last(k)
+    for k in range(2, T - 1):
+        chain_first(kg, far(k))
+    sum_group(0, 0, r.SV, r.SV2, q, NQ, chip_dev, "end")
+    sum_group(0, 1, r.SB, r.SB2, q, NQ, chip_dev, "end")
+    sum_group(1, 0, r.SV, r.SV3, t, T, row_dev, "start")
+    sum_group(1, 1, r.SB, r.SB3, t, T, row_dev, "start")
+    for k in range(H, T - 1):
+        rs_last(kd_, far(k))
+        rs_last(ku, far(k))
+    for k in range(T):
+        rs_mid(ko, far(k))
+    rs_mid(kq, 0)
     order = [2, 1] if T == 4 else list(range(1, T - 1))
-    for k in range(H, T - 1):
-        pair_last(k)
     for n, k in enumerate(order):
         pair_on(k)
-        if n > 0 or T != 4:
-            chain_on(kg, far(k))
-        else:
-            chain_on(kg, far(k))
-            for m in range(T):
-                rs_mid(ko, far(m))
-            rs_mid(kq, 0)
-    if T != 4:
-        for m in range(T):
-            rs_mid(ko, far(m))
-        rs_mid(kq, 0)
+        chain_on(kg, far(k))
+        if n == 0:
+            pair_mid(T - 1)
     for k in range(T - 1):
         rs_last(ko, far(k))
         chain_first(ko, far(k))
+    for k in range(H, T - 1):
+        chain_first(kd_, far(k))
+        chain_first(ku, far(k))
     for k in range(T - 1):
         chain_on(ko, far(k))
     rs_last(kd_, t)
@@ -940,7 +1045,7 @@
         "Wu": V((T, NQ, 2, R, HC), BF), "Wd": V((T, NQ, 2, R, HC), BF), "BU": V((T, 1, 2 * HC), F32), "vecs": V((8, D), F32), "segc": V((RW, 128), F32),
         "Q": V((RW, C), BF), "K": V((RW, C), BF), "V": V((RW, C), BF),
         "KT": V((C, RW), BF), "VT": V((C, RW), BF), "BIAS": V((RW, TB), F32),
-        "CT": V((C, TB), F32), "LSE": V((T, hp, TB), F32), "CXR": V((T, TB, C), BF),
+        "CT": V((C, TB), F32), "AM": V((T, hp, TB), F32), "AL": V((T, hp, TB), F32), "ACC": V((T, C, TB), F32), "CXR": V((T, TB, C), BF),
         "CTX": V((T, TB, C), BF), "FEED": V((2, TB, D), F32), "N1": V((TB, D), F32),
         "IV1": V((TB, 1), F32), "H1": V((TB, D), F32), "POOL": V((max(6, T), TB, D), BF),
         "MIDT": V((D, 2 * TB), BF), "PRE": V((TB, HC), F32), "ACT": V((T, 2 * TB, HC), BF),

time: 248 us -> 234 us (0.944)
  Pallas kernels: 247 us -> 233 us
    pallas_call x1, Pallas kernels: 244 us -> 230 us  [layer(): pl.pallas_call(functools.partial(layer_kernel, cf, names), out_shape=tupl...]
where the time goes in v3:
time: 234 us
  Pallas kernels  233 us (100%)
    pallas_call x1, Pallas kernels, layer(): pl.pallas_call(functools.partial(layer_kernel, cf, names), out_shape=tupl...  230 us

profile of v3, /device:TPU:0, one launch (start us, length us, event | category | flops | bytes accessed | tf_op | source)
XLA Modules:
  0.0 234.1 jit_solution(11047854390635519749)
XLA Ops:
  0.7 230.2 %layer.1 = (bf16[256,1024]{1,0:T(8,128)(2,1)}, bf16[256,1024]{1,0:T(8,128)(2,1)}, bf16[3,128,256]{2,1,0:T(8,128)(2,1)}, bf16[128,256]{1,0:T(8,128)(2,1)}, bf16[1...) custom-call(bf16[256,1024]{1,0:T(8,128)(2,1)} %refs_0_.1, ...), custom_call_target="tpu_custom_call" | custom-call | tf_op jit(solution)/shard_map/layer/pallas_call | solution.py:1086
  230.9 3.1 %tail.1 = (bf16[256,1024]{1,0:T(8,128)(2,1)}, bf16[256,1024]{1,0:T(8,128)(2,1)}, f32[3,128,256]{2,1,0:T(8,128)}, f32[2,256]{1,0:T(2,128)}, f32[256,128]{1,0:T(8,...) custom-call(bf16[256,1024]{1,0:T(8,128)(2,1)} %get-tuple-element.37., ...), custom_call_target="tpu_custom_call" | custom-call | tf_op jit(solution)/shard_map/tail/pallas_call | solution.py:1123

commit v4 on v3

--- a/solution.py
+++ b/solution.py
@@ -701,6 +701,7 @@
             rs_send(ku, tt, 0)
 
     H = T // 2
+    many = max(2, 256 // R)
 
     def far(k):
         return tp(T - 1 - k)
@@ -856,8 +857,45 @@
         def _():
             chain_first(kg, tt)
 
-    spin(0, H, attend_back)
-    part_last(ku, 0)
+    drain_gather(ko)
+    copy(r.RWO, r.RWO, r.tw_s.at[0], r.tw_r.at[0], partner).wait_send()
+
+
+    def out_back(tt):
+        def weight(g):
+            at = pl.ds(pl.multiple_of(g * many * R, 128), many * R)
+            y = lax.dot_general(
+                r.gtok[:, at], r.CTX[tt], (((0,), (0,)), ((), ())), preferred_element_type=F32
+            ).astype(BF)
+            r.Wo[tt, pl.ds(many * g, many)] = y.reshape(many, R, C)
+            for k in range(many // 2):
+                qq = g * (many // 2) + k
+                copy(r.Wo.at[tt, 2 * qq + oc], r.RWO.at[tt, qq], r.go_s.at[0], r.go_r.at[0], partner).start()
+
+        spin(0, DP // many, weight)
+
+    spin(0, T, out_back)
+
+    def attend_early(j):
+        attend_back(j)
+
+        @pl.when(j == 0)
+        def _():
+            part_last(ku, 0)
+
+    spin(0, H, attend_early)
+    copy(r.RWO, r.RWO, r.go_s.at[0], r.go_r.at[0], partner).wait_recv()
+
+    def out_join(k):
+        tt = tp(T - 1 - k)
+
+        def step(qq):
+            add(r.Wo.at[tt, 2 * qq + c], r.RWO.at[tt, qq])
+
+        spin(0, NQ, step)
+        rs_send(ko, tt, 0)
+
+    spin(0, T, out_join)
     for k in range(1, H):
         pair_mid(k)
     spin(H, T - 1, slot_weights)
@@ -882,43 +920,16 @@
 
     spin(0, T, input_rest)
     spin(T - 1, T, slot_weights)
+    for k in range(T):
+        rs_mid(ko, far(k))
     for k in range(H, T - 1):
         pair_mid(k)
     sum_core(2, r.SQ, r.SQ1, "start")
-    drain_gather(ko)
-    copy(r.RWO, r.RWO, r.tw_s.at[0], r.tw_r.at[0], partner).wait_send()
-
-    r.GFT[:, 0:TB] = r.gtok[...].astype(F32).T.astype(BF)
-
-    def out_back(tt):
-        def weight(qq):
-            at = pl.ds(pl.multiple_of(qq * 2 * R, 2 * R), 2 * R)
-            y = nn(r.GFT[at, 0:TB], r.CTX[tt]).astype(BF)
-            r.Wo[tt, pl.ds(2 * qq, 2)] = y.reshape(2, R, C)
-            copy(r.Wo.at[tt, 2 * qq + oc], r.RWO.at[tt, qq], r.go_s.at[0], r.go_r.at[0], partner).start()
-
-        spin(0, NQ, weight)
-
-    spin(0, T, out_back)
-
     pair_on(0)
-    copy(r.RWO, r.RWO, r.go_s.at[0], r.go_r.at[0], partner).wait_recv()
-
-    def out_join(k):
-        tt = tp(T - 1 - k)
-
-        def step(qq):
-            add(r.Wo.at[tt, 2 * qq + c], r.RWO.at[tt, qq])
-
-        spin(0, NQ, step)
-        rs_send(ko, tt, 0)
-
-    spin(0, T, out_join)
 
     copy(r.RQ, r.RQ, r.tw_s.at[1], r.tw_r.at[1], partner).wait_send()
     for s in range(S):
         ring_send(kq, 0, s, "drain")
-    many = max(2, 256 // R)
 
     def qkv_weight(g):
         cols = pl.ds(pl.multiple_of(g * many * R, 128), many * R)
@@ -943,6 +954,9 @@
     rs_send(kq, 0, 0)
     rs_send(kd_, t, 0)
     rs_send(ku, t, 0)
+    for k in range(T - 1):
+        rs_last(ko, far(k))
+        chain_first(ko, far(k))
     chain_on(kg, far(0))
     for k in range(1, H):
         pair_last(k)
@@ -953,24 +967,17 @@
     sum_group(1, 0, r.SV, r.SV3, t, T, row_dev, "start")
     sum_group(1, 1, r.SB, r.SB3, t, T, row_dev, "start")
     for k in range(H, T - 1):
-        rs_last(kd_, far(k))
-        rs_last(ku, far(k))
-    for k in range(T):
-        rs_mid(ko, far(k))
+        pair_last(k)
     rs_mid(kq, 0)
+    for k in range(H):
+        chain_on(ko, far(k))
     order = [2, 1] if T == 4 else list(range(1, T - 1))
     for n, k in enumerate(order):
         pair_on(k)
         chain_on(kg, far(k))
         if n == 0:
             pair_mid(T - 1)
-    for k in range(T - 1):
-        rs_last(ko, far(k))
-        chain_first(ko, far(k))
     for k in range(H, T - 1):
-        chain_first(kd_, far(k))
-        chain_first(ku, far(k))
-    for k in range(T - 1):
         chain_on(ko, far(k))
     rs_last(kd_, t)
     rs_last(ku, t)

time: 234 us -> 231 us (0.987); the launches traced: 234 us -> 226 us
  Pallas kernels: 233 us -> 225 us
    pallas_call x1, Pallas kernels: 230 us -> 222 us  [layer(): pl.pallas_call(functools.partial(layer_kernel, cf, names), out_shape=tupl...]
where the time goes in v4:
time: 231 us; the launch traced here: 226 us
  Pallas kernels  225 us (97%)
    pallas_call x1, Pallas kernels, layer(): pl.pallas_call(functools.partial(layer_kernel, cf, names), out_shape=tupl...  222 us

profile of v4, /device:TPU:0, one launch (start us, length us, event | category | flops | bytes accessed | tf_op | source)
XLA Modules:
  0.0 226.2 jit_solution(3340646945354513919)
XLA Ops:
  0.7 222.2 %layer.1 = (bf16[256,1024]{1,0:T(8,128)(2,1)}, bf16[256,1024]{1,0:T(8,128)(2,1)}, bf16[3,128,256]{2,1,0:T(8,128)(2,1)}, bf16[128,256]{1,0:T(8,128)(2,1)}, bf16[1...) custom-call(bf16[256,1024]{1,0:T(8,128)(2,1)} %refs_0_.1, ...), custom_call_target="tpu_custom_call" | custom-call | tf_op jit(solution)/shard_map/layer/pallas_call | solution.py:1093
  222.9 3.1 %tail.1 = (bf16[256,1024]{1,0:T(8,128)(2,1)}, bf16[256,1024]{1,0:T(8,128)(2,1)}, f32[3,128,256]{2,1,0:T(8,128)}, f32[2,256]{1,0:T(2,128)}, f32[256,128]{1,0:T(8,...) custom-call(bf16[256,1024]{1,0:T(8,128)(2,1)} %get-tuple-element.37., ...), custom_call_target="tpu_custom_call" | custom-call | tf_op jit(solution)/shard_map/tail/pallas_call | solution.py:1130

commit v5 on v4

--- a/solution.py
+++ b/solution.py
@@ -922,8 +922,6 @@
     spin(T - 1, T, slot_weights)
     for k in range(T):
         rs_mid(ko, far(k))
-    for k in range(H, T - 1):
-        pair_mid(k)
     sum_core(2, r.SQ, r.SQ1, "start")
     pair_on(0)
 
@@ -951,6 +949,8 @@
         add(r.Wq.at[2 * qq + c], r.RQ.at[qq])
 
     spin(0, NQ, q_join)
+    for k in range(H, T - 1):
+        pair_mid(k)
     rs_send(kq, 0, 0)
     rs_send(kd_, t, 0)
     rs_send(ku, t, 0)

time: 231 us -> 230 us (level)
  no operation moved by 1% of the time
where the time goes in v5:
time: 230 us; the launch traced here: 226 us
  Pallas kernels  225 us (98%)
    pallas_call x1, Pallas kernels, layer(): pl.pallas_call(functools.partial(layer_kernel, cf, names), out_shape=tupl...  222 us

profile of v5, /device:TPU:0, one launch (start us, length us, event | category | flops | bytes accessed | tf_op | source)
XLA Modules:
  0.0 226.2 jit_solution(13694520821633902013)
XLA Ops:
  0.7 222.2 %layer.1 = (bf16[256,1024]{1,0:T(8,128)(2,1)}, bf16[256,1024]{1,0:T(8,128)(2,1)}, bf16[3,128,256]{2,1,0:T(8,128)(2,1)}, bf16[128,256]{1,0:T(8,128)(2,1)}, bf16[1...) custom-call(bf16[256,1024]{1,0:T(8,128)(2,1)} %refs_0_.1, ...), custom_call_target="tpu_custom_call" | custom-call | tf_op jit(solution)/shard_map/layer/pallas_call | solution.py:1093
  222.9 3.1 %tail.1 = (bf16[256,1024]{1,0:T(8,128)(2,1)}, bf16[256,1024]{1,0:T(8,128)(2,1)}, f32[3,128,256]{2,1,0:T(8,128)}, f32[2,256]{1,0:T(2,128)}, f32[256,128]{1,0:T(8,...) custom-call(bf16[256,1024]{1,0:T(8,128)(2,1)} %get-tuple-element.37., ...), custom_call_target="tpu_custom_call" | custom-call | tf_op jit(solution)/shard_map/tail/pallas_call | solution.py:1130
